TPU v7x, 256 devices: a 8x8x2 block of a 8x8x16 slice. The times are simulated.
256 devices in a mesh: group: 2 (over z), expert: 128 (over x, y, core).
Axes of the slice: x: 8, y: 8, z: 2, core: 2. Of those that a mesh axis runs over, the one named last changes fastest.
The devices are a block of a 8x8x16 slice.
Arguments:
- query: bfloat16 [256, 2048], P(('group', 'expert')), parts along dimension 0, may hold values from -600 to 600
- key_new: bfloat16 [256, 2048], P(('group', 'expert')), parts along dimension 0, may hold values from -6 to 6
- value_new: bfloat16 [256, 2048], P(('group', 'expert')), parts along dimension 0, may hold values from -6 to 6
- key_cache: bfloat16 [256, 256, 2048], P(('group', 'expert')), parts along dimension 0, may hold values from -6 to 6
- value_cache: bfloat16 [256, 256, 2048], P(('group', 'expert')), parts along dimension 0, may hold values from -6 to 6
- lengths: int32 [256], P(('group', 'expert')), parts along dimension 0, may hold values from 1 to 256
- hidden: bfloat16 [256, 2048], P(('group', 'expert')), parts along dimension 0, may hold values from -6 to 6
- routes: int32 [256], P('group'), parts along dimension 0, may hold values from 0 to 31, as said below
- w_out: bfloat16 [2048, 2048], P(None, 'expert'), may hold values from -0.125 to 0.125
- ln_gain: bfloat16 [2048], replicated, may hold values from 0.099609375 to 1.8984375
- router: bfloat16 [2048, 32], replicated, may hold values from -0.125 to 0.125
- shared_up: bfloat16 [2048, 8192], P(None, 'expert'), may hold values from -0.125 to 0.125
- shared_down: bfloat16 [8192, 2048], P('expert'), may hold values from -0.0625 to 0.0625
- expert_up: bfloat16 [2048, 131072], P(None, 'expert'), may hold values from -0.125 to 0.125
- expert_down: bfloat16 [131072, 2048], P('expert'), may hold values from -0.09375 to 0.09375
Outputs:
- layer_out: bfloat16 [256, 2048], P(('group', 'expert')), parts along dimension 0
There are 2 independent parts, one for each index of `group`. A program takes and returns all parts, laid end to end along the dimension named above; an argument that names none is the same for every part. Nothing has to cross between parts.
Inputs may be any that keep to these rules, and one draw needn't show every extreme that they name: `routes`: no expert is named by more than 16 tokens of the group, and in every draw some expert is named by exactly 16.
All inputs are finite; a program needn't handle non-finite values.
Results may differ from a plain program's by a relative error of at most 0.0085.
Values may be sent and summed in bfloat16 or wider, within the bound.
A program may use at most 64 MiB of HBM per device.

v0:
```python
import math

import jax
import jax.numpy as jnp
from jax import lax
from jax.sharding import Mesh
from jax.sharding import PartitionSpec as P

D = 2048
HEADS = 16
HEAD_DIM = 128
FF = 4096
EXPERTS = 32
EXPERT = ("expert_0", "expert_1", "expert_2")
GROUP_EXPERT = ("group", "expert_0", "expert_1", "expert_2")


def in_one_piece(arrays, axis, dim, along):
    ends, at = ([], 0)
    for a in arrays[:-1]:
        at += a.shape[along]
        ends.append(at)
    both = jnp.concatenate(arrays, axis=along)
    return tuple(jnp.split(lax.all_gather(both, axis, axis=dim, tiled=True), ends, axis=along))


def joined_along(blocks, dim):
    blocks = jnp.moveaxis(blocks, 0, dim)
    shape = blocks.shape
    return blocks.reshape(*shape[:dim], shape[dim] * shape[dim + 1], *shape[dim + 2 :])


def all_blocks(x, axes, turns):
    blocks = x[None]
    for k in turns:
        blocks = lax.all_gather(blocks, axes[k], axis=0, tiled=True)
    held = [lax.axis_size(axes[k]) for k in reversed(turns)]
    blocks = blocks.reshape(*held, *x.shape)
    turned = sorted(range(len(turns)), key=lambda place: turns[len(turns) - 1 - place])
    return blocks.transpose(*turned, *range(len(turns), blocks.ndim)).reshape(-1, *x.shape)


def gathered_by_axis(x, axes, turns, dim):
    return joined_along(all_blocks(x, axes, turns), dim)


def sum_in_order(blocks, axes, turns):
    inside = blocks.shape[1:]
    blocks = blocks.reshape(*(lax.axis_size(a) for a in axes), *inside)
    blocks = jnp.moveaxis(blocks, turns, range(len(axes))).reshape(-1, *inside)
    for k in turns:
        blocks = lax.psum_scatter(blocks, axes[k], scatter_dimension=0, tiled=True)
    return blocks[0]


def in_blocks(x, dim, length):
    before, after = (x.shape[:dim], x.shape[dim + 1 :])
    return jnp.moveaxis(x.reshape(*before, length, -1, *after), dim, 0)


def summed_rows_2(x, axes, turns, dim):
    length = lax.axis_size(axes)
    return sum_in_order(in_blocks(x, dim, length), axes, turns)


def attend(query, key_new, value_new, key_cache, value_cache, lengths):
    seq_count = query.shape[0]
    cache_len = key_cache.shape[1]
    scale_factor = 1.0 / math.sqrt(HEAD_DIM)
    head_query = query.reshape(seq_count, HEADS, HEAD_DIM)
    head_keys = key_cache.reshape(seq_count, cache_len, HEADS, HEAD_DIM)
    head_values = value_cache.reshape(seq_count, cache_len, HEADS, HEAD_DIM)
    scores = (
        jnp.einsum("shd,schd->shc", head_query, head_keys, preferred_element_type=jnp.float32)
        * scale_factor
    )
    own_score = (
        jnp.einsum(
            "shd,shd->sh",
            head_query,
            key_new.reshape(seq_count, HEADS, HEAD_DIM),
            preferred_element_type=jnp.float32,
        )
        * scale_factor
    )
    positions = jnp.arange(cache_len, dtype=jnp.int32)
    scores = jnp.where(positions[None, None, :] < lengths[:, None, None], scores, -1e30)
    top_score = jnp.maximum(jnp.max(scores, axis=2), own_score)
    weights = jnp.exp(scores - top_score[:, :, None])
    own_weight = jnp.exp(own_score - top_score)
    normalizer = jnp.sum(weights, axis=2) + own_weight
    weights = (weights / normalizer[:, :, None]).astype(jnp.bfloat16)
    own_weight = (own_weight / normalizer).astype(jnp.bfloat16)
    mixed_values = jnp.einsum(
        "shc,schd->shd", weights, head_values, preferred_element_type=jnp.float32
    )
    mixed_values = mixed_values + own_weight.astype(jnp.float32)[:, :, None] * value_new.reshape(
        seq_count, HEADS, HEAD_DIM
    ).astype(jnp.float32)
    return mixed_values.reshape(seq_count, HEADS * HEAD_DIM).astype(jnp.bfloat16)


def body(
    query,
    key_new,
    value_new,
    key_cache,
    value_cache,
    lengths,
    hidden,
    routes,
    w_out,
    ln_gain,
    router,
    shared_up,
    shared_down,
    expert_up,
    expert_down,
):
    seq_count = query.shape[0]
    attended = attend(query, key_new, value_new, key_cache, value_cache, lengths)
    every_attended, every_hidden = in_one_piece((attended, hidden), EXPERT, 0, 1)
    projected = jnp.dot(every_attended, w_out, preferred_element_type=jnp.float32).astype(
        jnp.bfloat16
    )
    every_projected = gathered_by_axis(projected, EXPERT, (0, 1, 2), 1)
    residual = every_hidden.astype(jnp.float32) + every_projected.astype(jnp.float32)
    centered = residual - jnp.mean(residual, axis=1, keepdims=True)
    variance = jnp.mean(centered * centered, axis=1, keepdims=True)
    normed = (
        centered / jnp.sqrt(jnp.maximum(variance, 0.25)) * ln_gain.astype(jnp.float32)
    ).astype(jnp.bfloat16)
    logits = jnp.dot(normed, router, preferred_element_type=jnp.float32)
    all_experts = jnp.arange(EXPERTS, dtype=jnp.int32)
    chosen = jnp.sum(jnp.where(routes[:, None] == all_experts[None, :], logits, 0.0), axis=1)
    gate_value = jax.nn.sigmoid(chosen)
    shared_hidden = jax.nn.gelu(
        jnp.dot(normed, shared_up, preferred_element_type=jnp.float32), approximate=True
    ).astype(jnp.bfloat16)
    total_tokens = routes.shape[0]
    capacity = 4 * total_tokens // EXPERTS
    column_count = expert_up.shape[1]
    local_units = min(column_count, FF)
    local_experts = column_count // local_units
    device_index = lax.axis_index(EXPERT)
    first_expert = device_index * column_count // FF
    expert_ids = first_expert + jnp.arange(local_experts, dtype=jnp.int32)
    member = routes[:, None] == expert_ids[None, :]
    slot_rank = jnp.cumsum(member.astype(jnp.int32), axis=0) - 1
    slot_ids = jnp.arange(capacity, dtype=jnp.int32)
    placed = member[:, :, None] & (slot_rank[:, :, None] == slot_ids[None, None, :])
    picked = jnp.einsum(
        "skc,sd->kcd", placed.astype(jnp.bfloat16), normed, preferred_element_type=jnp.float32
    ).astype(jnp.bfloat16)
    up_local = expert_up.reshape(D, local_experts, local_units)
    inner_act = jax.nn.gelu(
        jnp.einsum("kcd,dkf->kcf", picked, up_local, preferred_element_type=jnp.float32),
        approximate=True,
    ).astype(jnp.bfloat16)
    down_local = expert_down.reshape(local_experts, local_units, D)
    result = jnp.einsum("kcf,kfd->kcd", inner_act, down_local, preferred_element_type=jnp.float32)
    spread = placed.astype(jnp.float32) * gate_value[:, None, None]
    summed = summed_rows_2(
        jnp.dot(shared_hidden, shared_down, preferred_element_type=jnp.float32)
        + jnp.einsum("skc,kcd->sd", spread, result, precision=lax.Precision.HIGHEST),
        EXPERT,
        (2, 0, 1),
        0,
    )
    own_residual = lax.dynamic_slice_in_dim(residual, device_index * seq_count, seq_count, 0)
    combined = own_residual + summed
    return combined.astype(jnp.bfloat16)


def solution(mesh):
    torus = Mesh(
        mesh.devices.reshape(mesh.shape["group"], 8, 8, 2),
        ("group", "expert_0", "expert_1", "expert_2"),
    )
    placed = (
        P(GROUP_EXPERT, None),
        P(GROUP_EXPERT, None),
        P(GROUP_EXPERT, None),
        P(GROUP_EXPERT, None, None),
        P(GROUP_EXPERT, None, None),
        P(GROUP_EXPERT),
        P(GROUP_EXPERT, None),
        P("group"),
        P(None, EXPERT),
        P(),
        P(),
        P(None, EXPERT),
        P(EXPERT, None),
        P(None, EXPERT),
        P(EXPERT, None),
    )
    return jax.shard_map(
        body, mesh=torus, in_specs=placed, out_specs=P(GROUP_EXPERT, None), check_vma=False
    )
```

profile of v0, /device:TPU:514, one launch (start us, length us, event | category | flops | bytes accessed | tf_op | source)
XLA Modules:
  0.0 316.4 jit_solution(2632683701685576357)
XLA Ops:
  6.5 0.0 copy-start
  6.6 0.1 all-gather.4.cloned.1.call-start
  6.6 1.5 copy.47
  8.2 0.0 copy-start.6
  8.9 0.9 fusion.47
  9.8 0.7 reduce.5
  10.5 0.7 reduce.6
  11.3 0.1 fusion.43
  11.4 0.1 fusion.46
  11.5 0.2 fusion.42
  11.7 0.1 fusion.49
  11.8 1.5 copy.52
  13.3 0.3 fusion.2
  13.6 0.1 fusion.50
  13.7 0.6 maximum_bitcast_fusion
  14.3 0.1 all-gather.4.cloned.1.call-update
  14.4 0.1 reduce-scatter.4.cloned.1.call-start
  14.5 0.1 copy.36
  14.7 0.2 reduce-window.7
  14.8 0.1 add_reduce_fusion
  14.9 96.7 %all-gather.4.cloned.1.call-done = bf16[128,1,4096]{2,1,0:T(2,128)(2,1)} async-done(((bf16[1,1,4096]{2,1,0:T(2,128)(2,1)}), bf16[128,1,4096]{2,1,0:T(2,128)(2,1)}) %all-gather.4.cloned.1.call-update) | async-done | bytes 1048592 | tf_op jit(solution)/shard_map/all_gather | solution.py:24
  111.6 2.7 copy.70
  114.3 0.2 convolution_convert_fusion.1
  114.6 22.2 %all-gather = bf16[1024,16]{0,1:T(8,128)(2,1)S(1)} all-gather(bf16[128,16]{0,1:T(8,128)(2,1)S(1)} %convolution_convert_fusion.1), channel_id=2, replica_groups=mesh['group'=2,'expert_0'=8,'expert_1'=8,'expert_2'=2] {'expert_0'}, dimensions={0}, use_global_device_ids=true | all-gather | bytes 36864 | tf_op jit(solution)/shard_map/all_gather | solution.py:36
  136.8 23.4 %all_gather.14 = bf16[64,128,16]{1,0,2:T(8,128)(2,1)S(1)} all-gather(bf16[8,128,16]{1,0,2:T(8,128)(2,1)S(1)} %bitcast.86), channel_id=1, replica_groups=mesh['group'=2,'expert_0'=8,'expert_1'=8,'expert_2'=2] {'expert_1'}, dimensions={0}, use_global_device_ids=true | all-gather | bytes 294912 | tf_op jit(solution)/shard_map/all_gather | solution.py:36
  160.1 2.2 all_gather.15
  162.3 0.3 copy.34
  162.6 0.3 copy.35
  163.0 0.2 fusion.57
  163.2 0.3 multiply_reduce_fusion
  163.4 0.2 multiply_convert_fusion
  163.7 1.0 fusion.1
  164.7 1.8 fusion.34
  166.5 3.1 fusion.12
  169.6 2.8 fusion.60
  172.4 2.0 convolution_add_fusion
  174.4 1.8 reshape_reshape.3
  176.3 1.6 copy.37
  177.9 0.1 reduce-scatter.4.cloned.1.call-update
  177.9 0.1 reduce-scatter.6.cloned.1.call-start
  178.0 10.8 %reduce-scatter.4.cloned.1.call-done = f32[64,1,2048]{2,0,1:T(8,128)} async-done(((f32[128,1,2048]{2,0,1:T(8,128)}), f32[64,1,2048]{2,0,1:T(8,128)}) %reduce-scatter.4.cloned.1.call-update) | async-done | bytes 524304 | tf_op jit(solution)/shard_map/reduce_scatter | solution.py:52
  188.8 0.1 reduce-scatter.6.cloned.1.call-update
  188.8 0.1 all-reduce.3.cloned.1.call-start
  188.9 42.0 %reduce-scatter.6.cloned.1.call-done = f32[8,1,2048]{2,0,1:T(8,128)} async-done(((f32[64,1,2048]{2,0,1:T(8,128)}), f32[8,1,2048]{2,0,1:T(8,128)}) %reduce-scatter.6.cloned.1.call-update) | async-done | bytes 65552 | tf_op jit(solution)/shard_map/reduce_scatter | solution.py:52
  230.9 0.1 all-reduce.3.cloned.1.call-update
  231.0 0.6 dynamic-slice
  231.5 76.3 %all-reduce.3.cloned.1.call-done = f32[8,1,2048]{2,0,1:T(8,128)} async-done(((f32[8,1,2048]{2,0,1:T(8,128)}), f32[8,1,2048]{2,0,1:T(8,128)}) %all-reduce.3.cloned.1.call-update) | async-done | bytes 65552
  307.8 2.0 fusion.45
  (25 shorter events, 0.1 us)
Async XLA Ops:
  6.5 158.1 %copy-start = (bf16[64,2048]{1,0:T(8,128)(2,1)S(1)}, bf16[64,2048]{1,0:T(8,128)(2,1)}, u32[]{:S(2)}) copy-start(bf16[64,2048]{1,0:T(8,128)(2,1)} %param.27) | copy-start | bytes 786436
  6.6 6.7 %copy-start.2 = (bf16[1,2048]{1,0:T(2,128)(2,1)S(1)}, bf16[1,2048]{1,0:T(2,128)(2,1)}, u32[]{:S(2)}) copy-start(bf16[1,2048]{1,0:T(2,128)(2,1)} %param.17) | copy-start | bytes 12292
  6.6 7.2 %copy-start.3 = (bf16[1,2048]{1,0:T(2,128)(2,1)S(1)}, bf16[1,2048]{1,0:T(2,128)(2,1)}, u32[]{:S(2)}) copy-start(bf16[1,2048]{1,0:T(2,128)(2,1)} %param.21) | copy-start | bytes 12292
  6.6 7.9 %copy-start.4 = (bf16[2048]{0:T(1024)(128)(2,1)S(1)}, bf16[2048]{0:T(1024)(128)(2,1)}, u32[]{:S(2)}) copy-start(bf16[2048]{0:T(1024)(128)(2,1)} %param.24) | copy-start | bytes 12292
  6.6 8.0 %copy-start.5 = (s32[128]{0:T(128)S(1)}, s32[128]{0:T(128)}, u32[]{:S(2)}) copy-start(s32[128]{0:T(128)} %param.22) | copy-start | bytes 1540
  6.6 105.0 %all-gather.4.cloned.1.call-start = ((), (), s32[]{:S(2)}) async-start(), calls=%async_computation.4 | async-start | bytes 2113536 | tf_op jit(solution)/shard_map/all_gather | solution.py:24
  8.2 106.2 %copy-start.6 = (bf16[2048,16]{0,1:T(8,128)(2,1)S(1)}, bf16[2048,16]{0,1:T(8,128)(2,1)}, u32[]{:S(2)}) copy-start(bf16[2048,16]{0,1:T(8,128)(2,1)} %param.23) | copy-start | bytes 196612
  14.4 174.4 %reduce-scatter.4.cloned.1.call-start = ((), (), s32[]{:S(2)}) async-start(), calls=%async_computation.2 | async-start | bytes 1572864 | tf_op jit(solution)/shard_map/reduce_scatter | solution.py:52
  162.3 1.3 copy-start.1
  172.4 58.6 %copy-start.7 = (u32[256]{0:T(256)S(1)}, u32[256]{0:T(256)}, u32[]{:S(2)}) copy-start(u32[256]{0:T(256)} %constant.84) | copy-start | bytes 3076
  177.9 53.0 %reduce-scatter.6.cloned.1.call-start = ((), (), s32[]{:S(2)}) async-start(), calls=%async_computation.3 | async-start | bytes 589824 | tf_op jit(solution)/shard_map/reduce_scatter | solution.py:52
  188.8 119.0 %all-reduce.3.cloned.1.call-start = ((), (), s32[]{:S(2)}) async-start(), calls=%async_computation.5 | async-start | bytes 131072
Sparse Core Ops, SparseCore 0:
  14.5 97.0 all-gather.3
  178.1 10.6 reduce-scatter.3
  191.3 39.5 reduce-scatter.5
  233.1 74.7 all-reduce.2
where the time goes:
time: 317 us; the launch traced here: 316 us
  waiting for transfers between devices  226 us (71%)
  blocking collectives  47.7 us (15%)
  between operations  14.1 us (4%)
  matrix products  12.2 us (4%)
  local copies, waits for them, and re-layouts  10.5 us (3%)
  other arithmetic  5.69 us (2%)
    all_gather x1, waiting for transfers between devices, in_one_piece(): lax.all_gather(both, axis, axis=dim, tiled=True)  96.7 us
    unnamed x5, waiting for transfers between devices  76.5 us
    reduce_scatter x2, waiting for transfers between devices, sum_in_order(): blocks = lax.psum_scatter(blocks, axes[k], scatter_dimension=0, tiled=True)  52.8 us
    all_gather x3, blocking collectives, all_blocks(): blocks = lax.all_gather(blocks, axes[k], axis=0, tiled=True)  47.7 us
  transfers between devices with their start and end apart: 4, of which 4 were waited for; matrix products, arithmetic and copies ran while one was open for 0% of the time, Pallas kernels for 0%

commit v1 on v0

v1 whole, which is shorter than its diff:
```python
import functools
import math

import jax
import jax.numpy as jnp
from jax import lax
from jax.experimental import pallas as pl
from jax.experimental.pallas import tpu as pltpu
from jax.sharding import Mesh
from jax.sharding import PartitionSpec as P

HEADS = 16
HEAD_DIM = 128
FF = 4096
RING = 8
TOKENS = 2 * RING * RING
HALF = RING * RING
EXPERT = ("expert_0", "expert_1", "expert_2")
GROUP_EXPERT = ("group", "expert_0", "expert_1", "expert_2")
MESH = pl.DeviceIdType.MESH
F32 = jnp.float32
BF16 = jnp.bfloat16
FAR_FIRST = (4, 3, 5, 2, 6, 1, 7)
NEAR_FIRST = (1, 7, 2, 6, 3, 5, 4)


def dot(a, b):
    return jnp.dot(a, b, preferred_element_type=F32)


def dot_nt(a, b):
    return lax.dot_general(a, b, (((1,), (1,)), ((), ())), preferred_element_type=F32)


def eye(n):
    return (
        lax.broadcasted_iota(jnp.int32, (n, n), 0) == lax.broadcasted_iota(jnp.int32, (n, n), 1)
    ).astype(BF16)


def diagonal(x):
    row = lax.broadcasted_iota(jnp.int32, (HEADS, HEAD_DIM), 0)
    out = jnp.zeros((HEADS, HEAD_DIM), F32)
    for h in range(HEADS):
        out = jnp.where(row == h, x[:, h * HEAD_DIM : (h + 1) * HEAD_DIM], out)
    return out


def kernel(*refs):
    ins, out_ref, (vm, sems) = refs[:15], refs[15], (refs[16:-8], refs[-8:])
    (
        q_v, kn_v, vn_v, k_v, v_v, len_v, hid_v, rt_v, wo_v, gain_v, router_v, sup_v, rhs, eup_v,
        edn_v, att, hid, pro, big, hid_t, gain_b, nat, res, proj_n, norm_t, up_t, wo_t, part, d_send,
        d_recv, p_send, p_recv, tok, t_recv, lhs,
    ) = vm
    load_sem, att_sem, hid_sem, pro_sem, d_sem, p_sem, t_sem, partner_sem = sems
    d_model = q_v.shape[1]
    shared_units = sup_v.shape[1]
    slots = TOKENS * 4 // 32

    x = lax.axis_index("expert_0")
    y = lax.axis_index("expert_1")
    core = lax.axis_index("expert_2")
    first = x * (1 - core) + y * core
    second = y * (1 - core) + x * core
    me = core * HALF + second * RING + first

    def on_first(k):
        return {
            "expert_0": (x + k * (1 - core)) % RING,
            "expert_1": (y + k * core) % RING,
            "expert_2": core,
        }

    def on_second(k):
        return {
            "expert_0": (x + k * core) % RING,
            "expert_1": (y + k * (1 - core)) % RING,
            "expert_2": core,
        }

    partner = {"expert_0": x, "expert_1": y, "expert_2": 1 - core}

    targets = (
        q_v, kn_v, vn_v, k_v, v_v, len_v, hid_v, rt_v, wo_v, gain_v, router_v, sup_v,
        rhs.at[pl.ds(0, shared_units)], eup_v, edn_v,
    )
    loads = [pltpu.make_async_copy(ins[i], targets[i], load_sem.at[i]) for i in range(15)]
    order = (0, 1, 2, 5, 6, 3, 4, 8, 11, 10, 9, 7, 12, 13, 14)
    for i in order:
        loads[i].start()

    barrier = pltpu.get_barrier_semaphore()
    for k in range(1, RING):
        pl.semaphore_signal(barrier, inc=1, device_id=on_first(k), device_id_type=MESH)
        pl.semaphore_signal(barrier, inc=1, device_id=on_second(k), device_id_type=MESH)
    pl.semaphore_signal(barrier, inc=1, device_id=partner, device_id_type=MESH)

    sent = []

    def send(src, dst, send_sem, recv_sem, to):
        copy = pltpu.make_async_remote_copy(
            src_ref=src, dst_ref=dst, send_sem=send_sem, recv_sem=recv_sem, device_id=to,
            device_id_type=MESH,
        )
        copy.start()
        sent.append(copy)

    def arrived(dst, send_sem, recv_sem):
        pltpu.make_async_remote_copy(
            src_ref=dst, dst_ref=dst, send_sem=send_sem, recv_sem=recv_sem, device_id=partner,
            device_id_type=MESH,
        ).wait_recv()

    def gather_1(buf, sem):
        slot = buf.at[pl.ds(me, 1)]
        for k in FAR_FIRST:
            send(slot, slot, sem.at[0, k], sem.at[1, k], on_first(k))

    def gather_2(buf, sem):
        for k in NEAR_FIRST:
            slot = core * HALF + second * RING + (first - k + RING) % RING
            arrived(buf.at[pl.ds(slot, 1)], sem.at[0, k], sem.at[1, k])
        row = buf.at[pl.ds(core * HALF + second * RING, RING)]
        for k in FAR_FIRST:
            send(row, row, sem.at[2, k], sem.at[3, k], on_second(k))
        send(row, row, sem.at[4, 0], sem.at[5, 0], partner)

    def gather_3(buf, sem):
        for k in NEAR_FIRST:
            row = buf.at[pl.ds(core * HALF + ((second - k + RING) % RING) * RING, RING)]
            arrived(row, sem.at[2, k], sem.at[3, k])
            send(row, row, sem.at[4, k], sem.at[5, k], partner)

    def gather_4(buf, sem):
        for k in (0,) + NEAR_FIRST:
            row = buf.at[pl.ds((1 - core) * HALF + ((first - k + RING) % RING) * RING, RING)]
            arrived(row, sem.at[4, k], sem.at[5, k])

    for i in (0, 1, 2, 5, 6):
        loads[i].wait()
    head_row = lax.broadcasted_iota(jnp.int32, (HEADS, d_model), 0)
    head_of_lane = lax.broadcasted_iota(jnp.int32, (HEADS, d_model), 1) // HEAD_DIM
    own_head = head_row == head_of_lane
    scale = 1.0 / math.sqrt(HEAD_DIM)

    def spread(ref):
        return jnp.broadcast_to(ref[...].astype(F32), (HEADS, d_model))

    hid_tile = diagonal(spread(hid_v))
    hid[pl.ds(me, 1)] = hid_tile.astype(BF16)[None]
    query = jnp.where(own_head, spread(q_v), 0.0)
    own_score = jnp.sum(query * spread(kn_v), axis=1, keepdims=True) * scale
    query = query.astype(BF16)
    loads[3].wait()
    scores = dot_nt(query, k_v[...]) * scale
    position = lax.broadcasted_iota(jnp.int32, scores.shape, 1)
    scores = jnp.where(position < jnp.broadcast_to(len_v[...], scores.shape), scores, -1e30)
    top = jnp.maximum(jnp.max(scores, axis=1, keepdims=True), own_score)
    weights = jnp.exp(scores - top)
    own_weight = jnp.exp(own_score - top)
    normalizer = jnp.sum(weights, axis=1, keepdims=True) + own_weight
    weights = (weights / normalizer).astype(BF16)
    own_weight = (own_weight / normalizer).astype(BF16).astype(F32)
    loads[4].wait()
    mixed = dot(weights, v_v[...]) + own_weight * spread(vn_v)
    att[pl.ds(me, 1)] = diagonal(mixed).astype(BF16)[None]

    pl.semaphore_wait(barrier, 2 * (RING - 1) + 1)
    gather_1(att, att_sem)
    gather_1(hid, hid_sem)

    loads[8].wait()
    wo_t[...] = dot_nt(eye(HEADS), wo_v[...]).astype(BF16)
    gather_2(att, att_sem)
    gather_2(hid, hid_sem)
    loads[11].wait()
    loads[10].wait()
    up_t[0:shared_units, :] = dot_nt(eye(shared_units), sup_v[...]).astype(BF16)
    experts = router_v.shape[1]
    up_t[shared_units:, :] = dot_nt(eye(experts), router_v[...]).astype(BF16)
    loads[9].wait()
    for h in range(HEADS):
        block = gain_v[:, h * HEAD_DIM : (h + 1) * HEAD_DIM].astype(F32)
        gain_b[h * HEAD_DIM : (h + 1) * HEAD_DIM, :] = jnp.broadcast_to(
            block, (HEAD_DIM, TOKENS)
        ).T
    loads[7].wait()
    nat_id = lax.broadcasted_iota(jnp.int32, (TOKENS, TOKENS), 0)
    lane = lax.broadcasted_iota(jnp.int32, (TOKENS, TOKENS), 1)
    lane_core, lane_second, lane_first = lane // HALF, (lane // RING) % RING, lane % RING
    lane_x = lane_first * (1 - lane_core) + lane_second * lane_core
    lane_y = lane_second * (1 - lane_core) + lane_first * lane_core
    to_slot = (nat_id == (lane_x * RING + lane_y) * 2 + lane_core).astype(BF16)
    routes = dot(
        jnp.broadcast_to(rt_v[...], (8, TOKENS)).astype(F32).astype(BF16), to_slot
    )[0:1].astype(jnp.int32)
    device = (x * RING + y) * 2 + core
    mine = device * eup_v.shape[1] // FF
    member = routes == mine
    rank = dot(
        jnp.broadcast_to(member.astype(F32), (8, TOKENS)).astype(BF16), (nat_id <= lane).astype(BF16)
    )[0:1].astype(jnp.int32) - 1
    slot_id = lax.broadcasted_iota(jnp.int32, (slots, TOKENS), 0)
    placed = jnp.where(
        jnp.broadcast_to(member, (slots, TOKENS))
        & (jnp.broadcast_to(rank, (slots, TOKENS)) == slot_id),
        1.0,
        0.0,
    )
    lhs[shared_units:, :] = placed.astype(BF16)

    gather_3(att, att_sem)
    gather_4(att, att_sem)
    big[...] = att[...].reshape(TOKENS * HEADS, HEAD_DIM).astype(F32)
    for h in range(HEADS):
        nat[:, h * HEAD_DIM : (h + 1) * HEAD_DIM] = big[pl.ds(h, TOKENS, stride=HEADS), :].astype(
            BF16
        )
    pro[pl.ds(me, 1)] = dot_nt(wo_t[...], nat[...]).astype(BF16)[None]
    gather_1(pro, pro_sem)
    gather_3(hid, hid_sem)
    gather_2(pro, pro_sem)
    gather_4(hid, hid_sem)
    big[...] = hid[...].reshape(TOKENS * HEADS, HEAD_DIM).astype(F32)
    for h in range(HEADS):
        hid_t[h * HEAD_DIM : (h + 1) * HEAD_DIM, :] = big[pl.ds(h, TOKENS, stride=HEADS), :].T
    gather_3(pro, pro_sem)
    gather_4(pro, pro_sem)

    cols = wo_v.shape[1]
    total = jnp.zeros((cols, TOKENS), F32)
    for n in range(TOKENS):
        n_core, n_y, n_x = n % 2, (n // 2) % RING, n // (2 * RING)
        slot = n_core * HALF + (n_x * RING + n_y if n_core else n_y * RING + n_x)
        rows = slice(n * cols, (n + 1) * cols)
        block = pro[slot]
        proj_n[rows, :] = block
        block = hid_t[rows, :] + block.astype(F32)
        res[rows, :] = block
        total = total + block
    mean = jnp.sum(total, axis=0, keepdims=True) / d_model
    total = jnp.zeros((HEAD_DIM, TOKENS), F32)
    for h in range(HEADS):
        centered = res[h * HEAD_DIM : (h + 1) * HEAD_DIM, :] - mean
        total = total + centered * centered
    variance = jnp.sum(total, axis=0, keepdims=True) / d_model
    inverse = 1.0 / jnp.sqrt(jnp.maximum(variance, 0.25))
    for h in range(HEADS):
        rows = slice(h * HEAD_DIM, (h + 1) * HEAD_DIM)
        norm_t[rows, :] = ((res[rows, :] - mean) * inverse * gain_b[rows, :]).astype(BF16)

    normed = norm_t[...]
    picked = dot_nt(placed.astype(BF16), normed).astype(BF16)
    both = dot(up_t[...], normed)
    lhs[0:shared_units, :] = jax.nn.gelu(both[0:shared_units], approximate=True).astype(BF16)
    expert_row = lax.broadcasted_iota(jnp.int32, (experts, TOKENS), 0)
    chosen = jnp.sum(
        jnp.where(jnp.broadcast_to(routes, (experts, TOKENS)) == expert_row, both[shared_units:], 0.0),
        axis=0,
        keepdims=True,
    )
    gate = 1.0 / (1.0 + jnp.exp(-chosen))
    slot_gate = jnp.sum(placed * gate, axis=1, keepdims=True)
    left = dot_nt(eye(TOKENS), lhs[...]).astype(BF16)
    nat[:, 0 : lhs.shape[0]] = left
    loads[13].wait()
    inner = jax.nn.gelu(dot(picked, eup_v[...]), approximate=True).astype(BF16)
    loads[14].wait()
    result = dot(inner, edn_v[...])
    loads[12].wait()
    rhs[shared_units:, :] = (result * slot_gate).astype(BF16)

    other = pl.multiple_of((1 - core) * HALF, HALF)
    mine_at = pl.multiple_of(core * HALF, HALF)
    depth = lhs.shape[0]
    step = 256
    theirs = nat[pl.ds(other, HALF), 0:depth]
    for at in range(0, d_model, step):
        piece = dot(theirs, rhs[:, at : at + step]).astype(BF16)
        d_send[:, :, at : at + step] = piece.reshape(RING, RING, step)
    for k in FAR_FIRST + (0,):
        block = (first + k) % RING
        send(d_send.at[block], d_recv.at[block], d_sem.at[0, k], d_sem.at[1, k], partner)
    ours = nat[pl.ds(mine_at, HALF), 0:depth]
    for at in range(0, d_model, step):
        part[:, at : at + step] = dot(ours, rhs[:, at : at + step])
    for k in FAR_FIRST + (0,):
        block = (second + k) % RING
        arrived(d_recv.at[block], d_sem.at[0, k], d_sem.at[1, k])
        rows = pl.ds(pl.multiple_of(block * RING, RING), RING)
        both_cores = part[rows, :] + d_recv[block].astype(F32)
        if k:
            p_send[k - 1] = both_cores.astype(BF16)
            send(p_send.at[k - 1], p_recv.at[k - 1], p_sem.at[0, k], p_sem.at[1, k], on_second(k))
        else:
            summed = both_cores
    own_column = (
        lax.broadcasted_iota(jnp.int32, (HEADS, TOKENS), 1) == me
    ).astype(BF16)
    own = hid_tile + diagonal(dot_nt(own_column, proj_n[...]))
    for k in NEAR_FIRST:
        arrived(p_recv.at[k - 1], p_sem.at[0, k], p_sem.at[1, k])
        summed = summed + p_recv[k - 1].astype(F32)
    for h in range(HEADS):
        tok[pl.ds(h, RING, stride=HEADS), :] = summed[:, h * HEAD_DIM : (h + 1) * HEAD_DIM]
    for k in FAR_FIRST:
        to = pl.multiple_of(((first + k) % RING) * HEADS, HEADS)
        send(tok.at[pl.ds(to, HEADS)], t_recv.at[k - 1], t_sem.at[0, k], t_sem.at[1, k], on_first(k))
    own = own + tok[pl.ds(pl.multiple_of(first * HEADS, HEADS), HEADS), :]
    for k in NEAR_FIRST:
        arrived(t_recv.at[k - 1], t_sem.at[0, k], t_sem.at[1, k])
        own = own + t_recv[k - 1]
    for h in range(HEADS):
        out_ref[:, h * HEAD_DIM : (h + 1) * HEAD_DIM] = own[h : h + 1, :].astype(BF16)
    for copy in sent:
        copy.wait_send()


def body(
    query, key_new, value_new, key_cache, value_cache, lengths, hidden, routes, w_out, ln_gain,
    router, shared_up, shared_down, expert_up, expert_down,
):
    key_cache = key_cache.reshape(key_cache.shape[1:])
    value_cache = value_cache.reshape(value_cache.shape[1:])
    lengths = lengths.reshape(1, 1)
    routes = routes.reshape(1, -1)
    ln_gain = ln_gain.reshape(1, -1)
    args = (
        query, key_new, value_new, key_cache, value_cache, lengths, hidden, routes, w_out, ln_gain,
        router, shared_up, shared_down, expert_up, expert_down,
    )
    d = query.shape[1]
    units = shared_up.shape[1]
    slots = TOKENS * 4 // 32
    tile = (TOKENS, HEADS, HEAD_DIM)

    def own(a):
        return pltpu.VMEM(a.shape, a.dtype)

    dma = pltpu.SemaphoreType.DMA
    scratch = [own(a) for a in args[:12]]
    scratch += [
        pltpu.VMEM((units + slots, d), BF16),
        own(expert_up),
        own(expert_down),
        pltpu.VMEM(tile, BF16),
        pltpu.VMEM(tile, BF16),
        pltpu.VMEM((TOKENS, w_out.shape[1], TOKENS), BF16),
        pltpu.VMEM((TOKENS * HEADS, HEAD_DIM), F32),
        pltpu.VMEM((d, TOKENS), F32),
        pltpu.VMEM((d, TOKENS), F32),
        pltpu.VMEM((TOKENS, d), BF16),
        pltpu.VMEM((d, TOKENS), F32),
        pltpu.VMEM((d, TOKENS), BF16),
        pltpu.VMEM((d, TOKENS), BF16),
        pltpu.VMEM((units + router.shape[1], d), BF16),
        pltpu.VMEM((w_out.shape[1], d), BF16),
        pltpu.VMEM((HALF, d), F32),
        pltpu.VMEM((RING, RING, d), BF16),
        pltpu.VMEM((RING, RING, d), BF16),
        pltpu.VMEM((RING - 1, RING, d), BF16),
        pltpu.VMEM((RING - 1, RING, d), BF16),
        pltpu.VMEM((RING * HEADS, HEAD_DIM), F32),
        pltpu.VMEM((RING - 1, HEADS, HEAD_DIM), F32),
        pltpu.VMEM((units + slots, TOKENS), BF16),
        dma((15,)),
        dma((6, RING)),
        dma((6, RING)),
        dma((6, RING)),
        dma((2, RING)),
        dma((2, RING)),
        dma((2, RING)),
        dma((1,)),
    ]
    return pl.pallas_call(
        kernel,
        out_shape=jax.ShapeDtypeStruct((1, d), BF16),
        in_specs=[pl.BlockSpec(memory_space=pl.ANY)] * 15,
        out_specs=pl.BlockSpec(memory_space=pltpu.VMEM),
        scratch_shapes=scratch,
        compiler_params=pltpu.CompilerParams(collective_id=0, has_side_effects=True),
        name="decode_layer",
    )(*args)


def solution(mesh):
    torus = Mesh(
        mesh.devices.reshape(mesh.shape["group"], RING, RING, 2),
        ("group", "expert_0", "expert_1", "expert_2"),
    )
    placed = (
        P(GROUP_EXPERT, None),
        P(GROUP_EXPERT, None),
        P(GROUP_EXPERT, None),
        P(GROUP_EXPERT, None, None),
        P(GROUP_EXPERT, None, None),
        P(GROUP_EXPERT),
        P(GROUP_EXPERT, None),
        P("group"),
        P(None, EXPERT),
        P(),
        P(),
        P(None, EXPERT),
        P(EXPERT, None),
        P(None, EXPERT),
        P(EXPERT, None),
    )
    return jax.shard_map(
        body, mesh=torus, in_specs=placed, out_specs=P(GROUP_EXPERT, None), check_vma=False
    )
```

time: 317 us -> 69.9 us (0.22)
  waiting for transfers between devices: 226 us -> 0 us
  Pallas kernels: 0 us -> 60.6 us
  blocking collectives: 47.7 us -> 0 us
  between operations: 14.1 us -> 0.66 us
  matrix products: 12.2 us -> 0 us
  other arithmetic: 5.69 us -> 0 us
    all_gather x1 -> x0, waiting for transfers between devices: 96.7 us -> none  [in_one_piece(): lax.all_gather(both, axis, axis=dim, tiled=True)]
    unnamed x5 -> x0, waiting for transfers between devices: 76.5 us -> none
    pallas_call x0 -> x1, Pallas kernels: none -> 60.6 us  [body(): pl.pallas_call(kernel, out_shape=jax.ShapeDtypeStruct((1, d), BF16), in_s...]
    reduce_scatter x2 -> x0, waiting for transfers between devices: 52.8 us -> none  [sum_in_order(): blocks = lax.psum_scatter(blocks, axes[k], scatter_dimension=0, tiled=True)]
    all_gather x3 -> x0, blocking collectives: 47.7 us -> none  [all_blocks(): blocks = lax.all_gather(blocks, axes[k], axis=0, tiled=True)]
    dot_general x8 -> x0, matrix products: 12.2 us -> none  [the longest x1 3.08 us: body(): jnp.einsum('kcd,dkf->kcf', picked, up_local, preferred_element_type=jnp.f...]
    another operation x4 -> x0, local copies, waits for them, and re-layouts: 5.07 us -> none  [the longest x2 3.44 us: sum_in_order(): blocks = blocks.reshape(*(lax.axis_size(a) for a in axes), *inside)]
    unnamed x21 -> x4, local copies, waits for them, and re-layouts: 4.81 us -> 7.04 us
  transfers between devices with their start and end apart: 4 -> 0, of which waited for: 4 -> 0; matrix products, arithmetic and copies ran while one was open for 0% -> 0% of each run, Pallas kernels for 0% -> 0%
where the time goes in v1:
time: 69.9 us; the launch traced here: 69.6 us
  Pallas kernels  60.6 us (87%)
  local copies, waits for them, and re-layouts  8.33 us (12%)
    pallas_call x1, Pallas kernels, body(): pl.pallas_call(kernel, out_shape=jax.ShapeDtypeStruct((1, d), BF16), in_s...  60.6 us
    unnamed x4, local copies, waits for them, and re-layouts  7.04 us

profile of v1, /device:TPU:514, one launch (start us, length us, event | category | flops | bytes accessed | tf_op | source)
XLA Modules:
  0.0 69.6 jit_solution(16201106090265165896)
XLA Ops:
  0.7 1.3 %reshape.19.refs_9_ = bf16[1,2048]{1,0:T(2,128)(2,1)} reshape(bf16[2048]{0:T(1024)(128)(2,1)} %param.24) | data formatting | bytes 8192 | tf_op jit(solution)/shard_map/reshape | solution.py:328
  1.9 1.8 %copy.16.refs_8_ = bf16[2048,16]{1,0:T(8,128)(2,1)} copy(bf16[2048,16]{0,1:T(8,128)(2,1)} %param.23) | data formatting | bytes 131072 | tf_op args[8]
  3.8 1.9 %copy.17.refs_10_ = bf16[2048,32]{1,0:T(8,128)(2,1)} copy(bf16[2048,32]{0,1:T(8,128)(2,1)} %param.25) | data formatting | bytes 262144 | tf_op args[10]
  5.7 2.0 %copy.18.refs_11_ = bf16[2048,64]{1,0:T(8,128)(2,1)} copy(bf16[2048,64]{0,1:T(8,128)(2,1)} %param.26) | data formatting | bytes 524288 | tf_op args[11]
  7.7 60.6 %decode_layer.1 = bf16[1,2048]{1,0:T(2,128)(2,1)} custom-call(bf16[1,2048]{1,0:T(2,128)(2,1)} %refs_0_.1, bf16[1,2048]{1,0:T(2,128)(2,1)} %refs_1_.1, bf16[1,2048]{1,0:T(2,128)(2,1)} %refs_2_.1, bf16[256,2048]{1,0:T(8,128)(2,1)} %bitcast.5, bf16[256,2048]{1,0:T(8,128)(2,1)} %bitcast.6, s32[1,1]{1,0:T(1,128)} %bitcast.4.refs_5_, bf16[1,2048]{1,0:T(2,128)(2,1)} %refs_6_.1, ...), custom_call_target="tpu_custom_call" | custom-call | tf_op jit(solution)/shard_map/decode_layer/pallas_call | solution.py:376
  68.3 1.3 %copy.21 = bf16[1,2048]{1,0:T(2,128)(2,1)} copy(bf16[1,2048]{1,0:T(2,128)(2,1)} %decode_layer.1) | data formatting | bytes 8192

commit v2 on v1

--- a/solution.py
+++ b/solution.py
@@ -49,13 +49,13 @@
 def kernel(*refs):
     ins, out_ref, (vm, sems) = refs[:15], refs[15], (refs[16:-8], refs[-8:])
     (
-        q_v, kn_v, vn_v, k_v, v_v, len_v, hid_v, rt_v, wo_v, gain_v, router_v, sup_v, rhs, eup_v,
-        edn_v, att, hid, pro, big, hid_t, gain_b, nat, res, proj_n, norm_t, up_t, wo_t, part, d_send,
-        d_recv, p_send, p_recv, tok, t_recv, lhs,
+        q_v, kn_v, vn_v, k_v, v_v, len_v, hid_v, rt_v, wo_t, gain_v, up_t, rhs, eup_v, edn_v, att, hid,
+        pro, big, hid_t, gain_b, nat, res, proj_n, norm_t, part, d_send, d_recv, p_send, p_recv, tok,
+        t_recv, lhs,
     ) = vm
     load_sem, att_sem, hid_sem, pro_sem, d_sem, p_sem, t_sem, partner_sem = sems
     d_model = q_v.shape[1]
-    shared_units = sup_v.shape[1]
+    experts, shared_units = ins[10].shape[0], ins[11].shape[0]
     slots = TOKENS * 4 // 32
 
     x = lax.axis_index("expert_0")
@@ -82,8 +82,8 @@
     partner = {"expert_0": x, "expert_1": y, "expert_2": 1 - core}
 
     targets = (
-        q_v, kn_v, vn_v, k_v, v_v, len_v, hid_v, rt_v, wo_v, gain_v, router_v, sup_v,
-        rhs.at[pl.ds(0, shared_units)], eup_v, edn_v,
+        q_v, kn_v, vn_v, k_v, v_v, len_v, hid_v, rt_v, wo_t, gain_v,
+        up_t.at[pl.ds(shared_units, experts)], up_t.at[pl.ds(0, shared_units)], rhs.at[pl.ds(0, shared_units)], eup_v, edn_v,
     )
     loads = [pltpu.make_async_copy(ins[i], targets[i], load_sem.at[i]) for i in range(15)]
     order = (0, 1, 2, 5, 6, 3, 4, 8, 11, 10, 9, 7, 12, 13, 14)
@@ -170,18 +170,11 @@
     gather_1(att, att_sem)
     gather_1(hid, hid_sem)
 
-    loads[8].wait()
-    wo_t[...] = dot_nt(eye(HEADS), wo_v[...]).astype(BF16)
     gather_2(att, att_sem)
     gather_2(hid, hid_sem)
-    loads[11].wait()
-    loads[10].wait()
-    up_t[0:shared_units, :] = dot_nt(eye(shared_units), sup_v[...]).astype(BF16)
-    experts = router_v.shape[1]
-    up_t[shared_units:, :] = dot_nt(eye(experts), router_v[...]).astype(BF16)
     loads[9].wait()
     for h in range(HEADS):
-        block = gain_v[:, h * HEAD_DIM : (h + 1) * HEAD_DIM].astype(F32)
+        block = gain_v[h : h + 1, :].astype(F32)
         gain_b[h * HEAD_DIM : (h + 1) * HEAD_DIM, :] = jnp.broadcast_to(
             block, (HEAD_DIM, TOKENS)
         ).T
@@ -217,6 +210,7 @@
         nat[:, h * HEAD_DIM : (h + 1) * HEAD_DIM] = big[pl.ds(h, TOKENS, stride=HEADS), :].astype(
             BF16
         )
+    loads[8].wait()
     pro[pl.ds(me, 1)] = dot_nt(wo_t[...], nat[...]).astype(BF16)[None]
     gather_1(pro, pro_sem)
     gather_3(hid, hid_sem)
@@ -228,7 +222,7 @@
     gather_3(pro, pro_sem)
     gather_4(pro, pro_sem)
 
-    cols = wo_v.shape[1]
+    cols = wo_t.shape[0]
     total = jnp.zeros((cols, TOKENS), F32)
     for n in range(TOKENS):
         n_core, n_y, n_x = n % 2, (n // 2) % RING, n // (2 * RING)
@@ -250,6 +244,8 @@
         rows = slice(h * HEAD_DIM, (h + 1) * HEAD_DIM)
         norm_t[rows, :] = ((res[rows, :] - mean) * inverse * gain_b[rows, :]).astype(BF16)
 
+    loads[10].wait()
+    loads[11].wait()
     normed = norm_t[...]
     picked = dot_nt(placed.astype(BF16), normed).astype(BF16)
     both = dot(up_t[...], normed)
@@ -325,13 +321,14 @@
     value_cache = value_cache.reshape(value_cache.shape[1:])
     lengths = lengths.reshape(1, 1)
     routes = routes.reshape(1, -1)
-    ln_gain = ln_gain.reshape(1, -1)
+    ln_gain = ln_gain.reshape(-1, HEAD_DIM)
+    w_out, router, shared_up = w_out.T, router.T, shared_up.T
     args = (
         query, key_new, value_new, key_cache, value_cache, lengths, hidden, routes, w_out, ln_gain,
         router, shared_up, shared_down, expert_up, expert_down,
     )
     d = query.shape[1]
-    units = shared_up.shape[1]
+    units = shared_up.shape[0]
     slots = TOKENS * 4 // 32
     tile = (TOKENS, HEADS, HEAD_DIM)
 
@@ -339,14 +336,15 @@
         return pltpu.VMEM(a.shape, a.dtype)
 
     dma = pltpu.SemaphoreType.DMA
-    scratch = [own(a) for a in args[:12]]
+    scratch = [own(a) for a in args[:10]]
     scratch += [
+        pltpu.VMEM((units + router.shape[0], d), BF16),
         pltpu.VMEM((units + slots, d), BF16),
         own(expert_up),
         own(expert_down),
         pltpu.VMEM(tile, BF16),
         pltpu.VMEM(tile, BF16),
-        pltpu.VMEM((TOKENS, w_out.shape[1], TOKENS), BF16),
+        pltpu.VMEM((TOKENS, w_out.shape[0], TOKENS), BF16),
         pltpu.VMEM((TOKENS * HEADS, HEAD_DIM), F32),
         pltpu.VMEM((d, TOKENS), F32),
         pltpu.VMEM((d, TOKENS), F32),
@@ -354,8 +352,6 @@
         pltpu.VMEM((d, TOKENS), F32),
         pltpu.VMEM((d, TOKENS), BF16),
         pltpu.VMEM((d, TOKENS), BF16),
-        pltpu.VMEM((units + router.shape[1], d), BF16),
-        pltpu.VMEM((w_out.shape[1], d), BF16),
         pltpu.VMEM((HALF, d), F32),
         pltpu.VMEM((RING, RING, d), BF16),
         pltpu.VMEM((RING, RING, d), BF16),

time: 69.9 us -> 63.1 us (0.903)
  local copies, waits for them, and re-layouts: 8.33 us -> 1.3 us
    unnamed x4 -> x1, local copies, waits for them, and re-layouts: 7.04 us -> 1.3 us
    reshape x1 -> x0, local copies, waits for them, and re-layouts: 1.29 us -> none  [body(): ln_gain = ln_gain.reshape(1, -1)]
where the time goes in v2:
time: 63.1 us; the launch traced here: 62.9 us
  Pallas kernels  61 us (97%)
  local copies, waits for them, and re-layouts  1.3 us (2%)
  between operations  0.66 us (1%)
    pallas_call x1, Pallas kernels, body(): pl.pallas_call(kernel, out_shape=jax.ShapeDtypeStruct((1, d), BF16), in_s...  61 us
    unnamed x1, local copies, waits for them, and re-layouts  1.3 us

profile of v2, /device:TPU:514, one launch (start us, length us, event | category | flops | bytes accessed | tf_op | source)
XLA Modules:
  0.0 62.9 jit_solution(4516008913052484165)
XLA Ops:
  0.7 61.0 %decode_layer.1 = bf16[1,2048]{1,0:T(2,128)(2,1)} custom-call(bf16[1,2048]{1,0:T(2,128)(2,1)} %refs_0_.1, bf16[1,2048]{1,0:T(2,128)(2,1)} %refs_1_.1, bf16[1,2048]{1,0:T(2,128)(2,1)} %refs_2_.1, bf16[256,2048]{1,0:T(8,128)(2,1)} %bitcast.9, bf16[256,2048]{1,0:T(8,128)(2,1)} %bitcast.10, s32[1,1]{1,0:T(1,128)} %bitcast.8.refs_5_, bf16[1,2048]{1,0:T(2,128)(2,1)} %refs_6_.1, ...), custom_call_target="tpu_custom_call" | custom-call | tf_op jit(solution)/shard_map/decode_layer/pallas_call | solution.py:372
  61.6 1.3 %copy.18 = bf16[1,2048]{1,0:T(2,128)(2,1)} copy(bf16[1,2048]{1,0:T(2,128)(2,1)} %decode_layer.1) | data formatting | bytes 8192

commit v3 on v2

--- a/solution.py
+++ b/solution.py
@@ -22,6 +22,10 @@
 BF16 = jnp.bfloat16
 FAR_FIRST = (4, 3, 5, 2, 6, 1, 7)
 NEAR_FIRST = (1, 7, 2, 6, 3, 5, 4)
+BY_HOPS = sorted(
+    ((k, j) for k in range(RING) for j in range(RING)),
+    key=lambda kj: min(kj[0], RING - kj[0]) + min(kj[1], RING - kj[1]),
+)
 
 
 def dot(a, b):
@@ -47,13 +51,14 @@
 
 
 def kernel(*refs):
-    ins, out_ref, (vm, sems) = refs[:15], refs[15], (refs[16:-8], refs[-8:])
+    ins, out_ref, (vm, sems) = refs[:15], refs[15], (refs[16:-17], refs[-17:])
     (
         q_v, kn_v, vn_v, k_v, v_v, len_v, hid_v, rt_v, wo_t, gain_v, up_t, rhs, eup_v, edn_v, att, hid,
         pro, big, hid_t, gain_b, nat, res, proj_n, norm_t, part, d_send, d_recv, p_send, p_recv, tok,
         t_recv, lhs,
     ) = vm
-    load_sem, att_sem, hid_sem, pro_sem, d_sem, p_sem, t_sem, partner_sem = sems
+    load_sem, hid_sem, d_sem, p_sem, t_sem = sems[:5]
+    att_sem, pro_sem = sems[5:11], sems[11:]
     d_model = q_v.shape[1]
     experts, shared_units = ins[10].shape[0], ins[11].shape[0]
     slots = TOKENS * 4 // 32
@@ -81,20 +86,20 @@
 
     partner = {"expert_0": x, "expert_1": y, "expert_2": 1 - core}
 
-    targets = (
-        q_v, kn_v, vn_v, k_v, v_v, len_v, hid_v, rt_v, wo_t, gain_v,
-        up_t.at[pl.ds(shared_units, experts)], up_t.at[pl.ds(0, shared_units)], rhs.at[pl.ds(0, shared_units)], eup_v, edn_v,
-    )
-    loads = [pltpu.make_async_copy(ins[i], targets[i], load_sem.at[i]) for i in range(15)]
-    order = (0, 1, 2, 5, 6, 3, 4, 8, 11, 10, 9, 7, 12, 13, 14)
-    for i in order:
-        loads[i].start()
-
     barrier = pltpu.get_barrier_semaphore()
     for k in range(1, RING):
         pl.semaphore_signal(barrier, inc=1, device_id=on_first(k), device_id_type=MESH)
         pl.semaphore_signal(barrier, inc=1, device_id=on_second(k), device_id_type=MESH)
     pl.semaphore_signal(barrier, inc=1, device_id=partner, device_id_type=MESH)
+
+    targets = (
+        q_v, kn_v, vn_v, k_v, v_v, len_v, hid_v, rt_v, wo_t, gain_v,
+        up_t.at[pl.ds(shared_units, experts)], up_t.at[pl.ds(0, shared_units)], rhs.at[pl.ds(0, shared_units)], eup_v, edn_v,
+    )
+    loads = [pltpu.make_async_copy(ins[i], targets[i], load_sem.at[i]) for i in range(15)]
+    order = (3, 0, 1, 2, 5, 6, 4, 9, 7, 8, 11, 10, 12, 13, 14)
+    for i in order:
+        loads[i].start()
 
     sent = []
 
@@ -111,6 +116,42 @@
             src_ref=dst, dst_ref=dst, send_sem=send_sem, recv_sem=recv_sem, device_id=partner,
             device_id_type=MESH,
         ).wait_recv()
+
+    def slot_of(k, second_k=0, of=core):
+        return (
+            of * HALF + ((second - second_k + RING) % RING) * RING + (first - k + RING) % RING
+        )
+
+    def pass_on(buf, sems, k):
+        tile = buf.at[pl.ds(slot_of(k), 1)]
+        for j in FAR_FIRST:
+            send(tile, tile, sems[2].at[k, j], sems[3].at[k, j], on_second(j))
+        send(tile, tile, sems[4].at[k, 0], sems[5].at[k, 0], partner)
+
+    def tiles_1(buf, sems):
+        tile = buf.at[pl.ds(me, 1)]
+        for k in FAR_FIRST:
+            send(tile, tile, sems[0].at[0, k], sems[1].at[0, k], on_first(k))
+        pass_on(buf, sems, 0)
+
+    def tiles_2(buf, sems):
+        for k in NEAR_FIRST:
+            arrived(buf.at[pl.ds(slot_of(k), 1)], sems[0].at[0, k], sems[1].at[0, k])
+            pass_on(buf, sems, k)
+
+    def tiles_3(buf, sems):
+        for k, j in BY_HOPS:
+            if j:
+                tile = buf.at[pl.ds(slot_of(k, j), 1)]
+                arrived(tile, sems[2].at[k, j], sems[3].at[k, j])
+                send(tile, tile, sems[4].at[k, j], sems[5].at[k, j], partner)
+
+    def tiles_4(buf, sems):
+        for k, j in BY_HOPS:
+            slot = (
+                (1 - core) * HALF + ((first - j + RING) % RING) * RING + (second - k + RING) % RING
+            )
+            arrived(buf.at[pl.ds(slot, 1)], sems[4].at[k, j], sems[5].at[k, j])
 
     def gather_1(buf, sem):
         slot = buf.at[pl.ds(me, 1)]
@@ -167,11 +208,9 @@
     att[pl.ds(me, 1)] = diagonal(mixed).astype(BF16)[None]
 
     pl.semaphore_wait(barrier, 2 * (RING - 1) + 1)
-    gather_1(att, att_sem)
+    tiles_1(att, att_sem)
     gather_1(hid, hid_sem)
 
-    gather_2(att, att_sem)
-    gather_2(hid, hid_sem)
     loads[9].wait()
     for h in range(HEADS):
         block = gain_v[h : h + 1, :].astype(F32)
@@ -203,24 +242,37 @@
     )
     lhs[shared_units:, :] = placed.astype(BF16)
 
-    gather_3(att, att_sem)
-    gather_4(att, att_sem)
-    big[...] = att[...].reshape(TOKENS * HEADS, HEAD_DIM).astype(F32)
-    for h in range(HEADS):
-        nat[:, h * HEAD_DIM : (h + 1) * HEAD_DIM] = big[pl.ds(h, TOKENS, stride=HEADS), :].astype(
-            BF16
-        )
+    tiles_2(att, att_sem)
+    tiles_3(att, att_sem)
+    gather_2(hid, hid_sem)
+
+    def relayout(buf, at):
+        at = pl.multiple_of(at, HALF)
+        rows = pl.ds(pl.multiple_of(at * HEADS, HALF * HEADS), HALF * HEADS)
+        big[rows, :] = buf[pl.ds(at, HALF)].reshape(HALF * HEADS, HEAD_DIM).astype(F32)
+
+    def att_rows(at):
+        relayout(att, at)
+        at = pl.multiple_of(at, HALF)
+        for h in range(HEADS):
+            nat[pl.ds(at, HALF), h * HEAD_DIM : (h + 1) * HEAD_DIM] = big[
+                pl.ds(at * HEADS + h, HALF, stride=HEADS), :
+            ].astype(BF16)
+
+    att_rows(core * HALF)
+    tiles_4(att, att_sem)
+    att_rows((1 - core) * HALF)
     loads[8].wait()
     pro[pl.ds(me, 1)] = dot_nt(wo_t[...], nat[...]).astype(BF16)[None]
-    gather_1(pro, pro_sem)
+    tiles_1(pro, pro_sem)
+    tiles_2(pro, pro_sem)
     gather_3(hid, hid_sem)
-    gather_2(pro, pro_sem)
     gather_4(hid, hid_sem)
     big[...] = hid[...].reshape(TOKENS * HEADS, HEAD_DIM).astype(F32)
     for h in range(HEADS):
         hid_t[h * HEAD_DIM : (h + 1) * HEAD_DIM, :] = big[pl.ds(h, TOKENS, stride=HEADS), :].T
-    gather_3(pro, pro_sem)
-    gather_4(pro, pro_sem)
+    tiles_3(pro, pro_sem)
+    tiles_4(pro, pro_sem)
 
     cols = wo_t.shape[0]
     total = jnp.zeros((cols, TOKENS), F32)
@@ -362,13 +414,11 @@
         pltpu.VMEM((units + slots, TOKENS), BF16),
         dma((15,)),
         dma((6, RING)),
-        dma((6, RING)),
-        dma((6, RING)),
         dma((2, RING)),
         dma((2, RING)),
         dma((2, RING)),
-        dma((1,)),
     ]
+    scratch += 2 * (2 * [dma((1, RING))] + 4 * [dma((RING, RING))])
     return pl.pallas_call(
         kernel,
         out_shape=jax.ShapeDtypeStruct((1, d), BF16),

time: 63.1 us -> 65.7 us (1.041)
  Pallas kernels: 61 us -> 63.6 us
    pallas_call x1, Pallas kernels: 61 us -> 63.6 us  [body(): pl.pallas_call(kernel, out_shape=jax.ShapeDtypeStruct((1, d), BF16), in_s...]
where the time goes in v3:
time: 65.7 us; the launch traced here: 65.5 us
  Pallas kernels  63.6 us (97%)
  local copies, waits for them, and re-layouts  1.3 us (2%)
  between operations  0.66 us (1%)
    pallas_call x1, Pallas kernels, body(): pl.pallas_call(kernel, out_shape=jax.ShapeDtypeStruct((1, d), BF16), in_s...  63.6 us

profile of v3, /device:TPU:514, one launch (start us, length us, event | category | flops | bytes accessed | tf_op | source)
XLA Modules:
  0.0 65.5 jit_solution(326336899132115961)
XLA Ops:
  0.7 63.6 %decode_layer.1 = bf16[1,2048]{1,0:T(2,128)(2,1)} custom-call(bf16[1,2048]{1,0:T(2,128)(2,1)} %refs_0_.1, bf16[1,2048]{1,0:T(2,128)(2,1)} %refs_1_.1, bf16[1,2048]{1,0:T(2,128)(2,1)} %refs_2_.1, bf16[256,2048]{1,0:T(8,128)(2,1)} %bitcast.9, bf16[256,2048]{1,0:T(8,128)(2,1)} %bitcast.10, s32[1,1]{1,0:T(1,128)} %bitcast.8.refs_5_, bf16[1,2048]{1,0:T(2,128)(2,1)} %refs_6_.1, ...), custom_call_target="tpu_custom_call" | custom-call | tf_op jit(solution)/shard_map/decode_layer/pallas_call | solution.py:422
  64.2 1.3 %copy.18 = bf16[1,2048]{1,0:T(2,128)(2,1)} copy(bf16[1,2048]{1,0:T(2,128)(2,1)} %decode_layer.1) | data formatting | bytes 8192

commit v4 on v3

v4 whole, which is shorter than its diff:
```python
import functools
import math

import jax
import jax.numpy as jnp
from jax import lax
from jax.experimental import pallas as pl
from jax.experimental.pallas import tpu as pltpu
from jax.sharding import Mesh
from jax.sharding import PartitionSpec as P

HEADS = 16
HEAD_DIM = 128
FF = 4096
RING = 8
TOKENS = 2 * RING * RING
HALF = RING * RING
EXPERT = ("expert_0", "expert_1", "expert_2")
GROUP_EXPERT = ("group", "expert_0", "expert_1", "expert_2")
MESH = pl.DeviceIdType.MESH
F32 = jnp.float32
BF16 = jnp.bfloat16
FAR_FIRST = (4, 3, 5, 2, 6, 1, 7)
NEAR_FIRST = (1, 7, 2, 6, 3, 5, 4)


def dot(a, b):
    return jnp.dot(a, b, preferred_element_type=F32)


def dot_nt(a, b):
    return lax.dot_general(a, b, (((1,), (1,)), ((), ())), preferred_element_type=F32)


def eye(n):
    return (
        lax.broadcasted_iota(jnp.int32, (n, n), 0) == lax.broadcasted_iota(jnp.int32, (n, n), 1)
    ).astype(BF16)


def diagonal(x):
    row = lax.broadcasted_iota(jnp.int32, (HEADS, HEAD_DIM), 0)
    out = jnp.zeros((HEADS, HEAD_DIM), F32)
    for h in range(HEADS):
        out = jnp.where(row == h, x[:, h * HEAD_DIM : (h + 1) * HEAD_DIM], out)
    return out


def kernel(*refs):
    ins, out_ref, vm, sems = refs[:15], refs[15], refs[16:-9], refs[-9:]
    (
        rows_v, k_v, v_v, len_v, rt_v, wo_t, gain_v, up_t, rhs, eup_v, edn_v, att, hid, pro, big,
        hid_t, gain_b, nat, res, proj_n, norm_t, part, p_send, p_recv, tok, t_recv, lhs,
    ) = vm
    load_sem, att_sem, hid_sem, pro_sem, down_sem, act_sem, slot_sem, p_sem, t_sem = sems
    d_model = rows_v.shape[2]
    experts, shared_units = ins[10].shape[0], ins[11].shape[0]
    slots = TOKENS * 4 // 32

    x = lax.axis_index("expert_0")
    y = lax.axis_index("expert_1")
    core = lax.axis_index("expert_2")
    first = x * (1 - core) + y * core
    second = y * (1 - core) + x * core
    me = core * HALF + second * RING + first

    def on_first(k):
        return {
            "expert_0": (x + k * (1 - core)) % RING,
            "expert_1": (y + k * core) % RING,
            "expert_2": core,
        }

    def on_second(k):
        return {
            "expert_0": (x + k * core) % RING,
            "expert_1": (y + k * (1 - core)) % RING,
            "expert_2": core,
        }

    partner = {"expert_0": x, "expert_1": y, "expert_2": 1 - core}

    barrier = pltpu.get_barrier_semaphore()
    for k in range(1, RING):
        pl.semaphore_signal(barrier, inc=1, device_id=on_first(k), device_id_type=MESH)
        pl.semaphore_signal(barrier, inc=1, device_id=on_second(k), device_id_type=MESH)
    pl.semaphore_signal(barrier, inc=1, device_id=partner, device_id_type=MESH)

    query_v, key_v, value_v, hid_v = (rows_v.at[i] for i in range(4))

    def load(i, target, sem):
        copy = pltpu.make_async_copy(ins[i], target, load_sem.at[sem])
        copy.start()
        return copy

    for i, row in ((0, query_v), (1, key_v), (2, value_v), (6, hid_v)):
        load(i, row, 0)
    rows_load = pltpu.make_async_copy(rows_v, rows_v, load_sem.at[0])
    k_load = load(3, k_v, 1)
    len_load = load(5, len_v, 2)
    v_load = load(4, v_v, 3)
    gain_load = load(9, gain_v, 4)
    rt_load = load(7, rt_v, 5)
    down_load = load(12, rhs.at[pl.ds(0, shared_units)], 6)
    wo_load = load(8, wo_t, 7)
    load(11, up_t.at[pl.ds(0, shared_units)], 8)
    load(10, up_t.at[pl.ds(shared_units, experts)], 8)
    up_load = pltpu.make_async_copy(up_t, up_t, load_sem.at[8])
    eup_load = load(13, eup_v, 9)
    edn_load = load(14, edn_v, 10)

    def send(src, dst, send_sem, recv_sem, to):
        copy = pltpu.make_async_remote_copy(
            src_ref=src, dst_ref=dst, send_sem=send_sem, recv_sem=recv_sem, device_id=to,
            device_id_type=MESH,
        )
        copy.start()

    def wait_for(ref, sem):
        pltpu.make_async_copy(ref, ref, sem).wait()

    def slot_of(k):
        return core * HALF + second * RING + (first - k + RING) % RING

    def row_of(second_k, of=core):
        return pl.ds(of * HALF + ((second - second_k + RING) % RING) * RING, RING)

    def pass_on(buf, sem, k):
        tile = buf.at[pl.ds(slot_of(k), 1)]
        for j in FAR_FIRST:
            send(tile, tile, sem.at[0], sem.at[8 + j], on_second(j))

    def tiles_1(buf, sem):
        tile = buf.at[pl.ds(me, 1)]
        for k in FAR_FIRST:
            send(tile, tile, sem.at[0], sem.at[1 + k], on_first(k))
        pass_on(buf, sem, 0)

    def tiles_2(buf, sem):
        for k in NEAR_FIRST:
            wait_for(buf.at[pl.ds(slot_of(k), 1)], sem.at[1 + k])
            pass_on(buf, sem, k)
        row = buf.at[row_of(0)]
        send(row, row, sem.at[0], sem.at[1], partner)

    def tiles_3(buf, sem):
        for j in NEAR_FIRST:
            row = buf.at[row_of(j)]
            wait_for(row, sem.at[8 + j])
            send(row, row, sem.at[0], sem.at[1], partner)

    def tiles_4(buf, sem):
        wait_for(buf.at[pl.ds((1 - core) * HALF, HALF)], sem.at[1])

    def steps_1(buf, sem):
        tile = buf.at[pl.ds(me, 1)]
        for k in FAR_FIRST:
            send(tile, tile, sem.at[0], sem.at[1], on_first(k))

    def steps_2(buf, sem):
        wait_for(buf.at[pl.ds(0, RING - 1)], sem.at[1])
        row = buf.at[row_of(0)]
        for k in FAR_FIRST:
            send(row, row, sem.at[0], sem.at[2], on_second(k))

    def steps_3(buf, sem):
        wait_for(buf.at[pl.ds(0, HALF - RING)], sem.at[2])
        half = buf.at[pl.ds(core * HALF, HALF)]
        send(half, half, sem.at[0], sem.at[3], partner)

    def steps_4(buf, sem):
        wait_for(buf.at[pl.ds((1 - core) * HALF, HALF)], sem.at[3])

    rows_load.wait()
    head_row = lax.broadcasted_iota(jnp.int32, (HEADS, d_model), 0)
    head_of_lane = lax.broadcasted_iota(jnp.int32, (HEADS, d_model), 1) // HEAD_DIM
    own_head = head_row == head_of_lane
    scale = 1.0 / math.sqrt(HEAD_DIM)

    def spread(ref):
        return jnp.broadcast_to(ref[...].astype(F32), (HEADS, d_model))

    hid_tile = diagonal(spread(hid_v))
    hid[pl.ds(me, 1)] = hid_tile.astype(BF16)[None]
    query = jnp.where(own_head, spread(query_v), 0.0)
    own_score = jnp.sum(query * spread(key_v), axis=1, keepdims=True) * scale
    query = query.astype(BF16)
    k_load.wait()
    len_load.wait()
    scores = dot_nt(query, k_v[...]) * scale
    position = lax.broadcasted_iota(jnp.int32, scores.shape, 1)
    scores = jnp.where(position < jnp.broadcast_to(len_v[...], scores.shape), scores, -1e30)
    top = jnp.maximum(jnp.max(scores, axis=1, keepdims=True), own_score)
    weights = jnp.exp(scores - top)
    own_weight = jnp.exp(own_score - top)
    normalizer = jnp.sum(weights, axis=1, keepdims=True) + own_weight
    weights = (weights / normalizer).astype(BF16)
    own_weight = (own_weight / normalizer).astype(BF16).astype(F32)
    v_load.wait()
    mixed = dot(weights, v_v[...]) + own_weight * spread(value_v)
    att[pl.ds(me, 1)] = diagonal(mixed).astype(BF16)[None]

    pl.semaphore_wait(barrier, 2 * (RING - 1) + 1)
    tiles_1(att, att_sem)
    steps_1(hid, hid_sem)

    gain_load.wait()
    for h in range(HEADS):
        block = gain_v[h : h + 1, :].astype(F32)
        gain_b[h * HEAD_DIM : (h + 1) * HEAD_DIM, :] = jnp.broadcast_to(
            block, (HEAD_DIM, TOKENS)
        ).T
    rt_load.wait()
    nat_id = lax.broadcasted_iota(jnp.int32, (TOKENS, TOKENS), 0)
    lane = lax.broadcasted_iota(jnp.int32, (TOKENS, TOKENS), 1)
    lane_core, lane_second, lane_first = lane // HALF, (lane // RING) % RING, lane % RING
    lane_x = lane_first * (1 - lane_core) + lane_second * lane_core
    lane_y = lane_second * (1 - lane_core) + lane_first * lane_core
    to_slot = (nat_id == (lane_x * RING + lane_y) * 2 + lane_core).astype(BF16)
    routes = dot(
        jnp.broadcast_to(rt_v[...], (8, TOKENS)).astype(F32).astype(BF16), to_slot
    )[0:1].astype(jnp.int32)
    device = (x * RING + y) * 2 + core
    mine = device * eup_v.shape[1] // FF
    member = routes == mine
    rank = dot(
        jnp.broadcast_to(member.astype(F32), (8, TOKENS)).astype(BF16), (nat_id <= lane).astype(BF16)
    )[0:1].astype(jnp.int32) - 1
    slot_id = lax.broadcasted_iota(jnp.int32, (slots, TOKENS), 0)
    placed = jnp.where(
        jnp.broadcast_to(member, (slots, TOKENS))
        & (jnp.broadcast_to(rank, (slots, TOKENS)) == slot_id),
        1.0,
        0.0,
    )
    placed_at, depth = 2 * shared_units, lhs.shape[0]
    lhs[placed_at : placed_at + slots, :] = placed.astype(BF16)
    lhs[placed_at + slots :, :] = placed.astype(BF16)
    down_load.wait()
    send(
        rhs.at[pl.ds(0, shared_units)], rhs.at[pl.ds(shared_units, shared_units)], down_sem.at[0],
        down_sem.at[1], partner,
    )

    tiles_2(att, att_sem)
    tiles_3(att, att_sem)
    steps_2(hid, hid_sem)

    def relayout(buf, at):
        at = pl.multiple_of(at, HALF)
        rows = pl.ds(pl.multiple_of(at * HEADS, HALF * HEADS), HALF * HEADS)
        big[rows, :] = buf[pl.ds(at, HALF)].reshape(HALF * HEADS, HEAD_DIM).astype(F32)

    def att_rows(at):
        relayout(att, at)
        at = pl.multiple_of(at, HALF)
        for h in range(HEADS):
            nat[pl.ds(at, HALF), h * HEAD_DIM : (h + 1) * HEAD_DIM] = big[
                pl.ds(at * HEADS + h, HALF, stride=HEADS), :
            ].astype(BF16)

    att_rows(core * HALF)
    tiles_4(att, att_sem)
    att_rows((1 - core) * HALF)
    wo_load.wait()
    pro[pl.ds(me, 1)] = dot_nt(wo_t[...], nat[...]).astype(BF16)[None]
    tiles_1(pro, pro_sem)
    tiles_2(pro, pro_sem)
    steps_3(hid, hid_sem)
    steps_4(hid, hid_sem)
    big[...] = hid[...].reshape(TOKENS * HEADS, HEAD_DIM).astype(F32)
    for h in range(HEADS):
        hid_t[h * HEAD_DIM : (h + 1) * HEAD_DIM, :] = big[pl.ds(h, TOKENS, stride=HEADS), :].T
    tiles_3(pro, pro_sem)
    tiles_4(pro, pro_sem)

    cols = wo_t.shape[0]
    total = jnp.zeros((cols, TOKENS), F32)
    for n in range(TOKENS):
        n_core, n_y, n_x = n % 2, (n // 2) % RING, n // (2 * RING)
        slot = n_core * HALF + (n_x * RING + n_y if n_core else n_y * RING + n_x)
        rows = slice(n * cols, (n + 1) * cols)
        block = pro[slot]
        proj_n[rows, :] = block
        block = hid_t[rows, :] + block.astype(F32)
        res[rows, :] = block
        total = total + block
    mean = jnp.sum(total, axis=0, keepdims=True) / d_model
    total = jnp.zeros((HEAD_DIM, TOKENS), F32)
    for h in range(HEADS):
        centered = res[h * HEAD_DIM : (h + 1) * HEAD_DIM, :] - mean
        total = total + centered * centered
    variance = jnp.sum(total, axis=0, keepdims=True) / d_model
    inverse = 1.0 / jnp.sqrt(jnp.maximum(variance, 0.25))
    for h in range(HEADS):
        rows = slice(h * HEAD_DIM, (h + 1) * HEAD_DIM)
        norm_t[rows, :] = ((res[rows, :] - mean) * inverse * gain_b[rows, :]).astype(BF16)

    up_load.wait()
    normed = norm_t[...]
    both = dot(up_t[...], normed)
    lhs[0:shared_units, :] = jax.nn.gelu(both[0:shared_units], approximate=True).astype(BF16)
    send(
        lhs.at[pl.ds(0, shared_units)], lhs.at[pl.ds(shared_units, shared_units)], act_sem.at[0],
        act_sem.at[1], partner,
    )
    picked = dot_nt(placed.astype(BF16), normed).astype(BF16)
    expert_row = lax.broadcasted_iota(jnp.int32, (experts, TOKENS), 0)
    chosen = jnp.sum(
        jnp.where(jnp.broadcast_to(routes, (experts, TOKENS)) == expert_row, both[shared_units:], 0.0),
        axis=0,
        keepdims=True,
    )
    gate = 1.0 / (1.0 + jnp.exp(-chosen))
    slot_gate = jnp.sum(placed * gate, axis=1, keepdims=True)
    eup_load.wait()
    inner = jax.nn.gelu(dot(picked, eup_v[...]), approximate=True).astype(BF16)
    edn_load.wait()
    wide = d_model // 2
    theirs = placed_at + slots
    for i in range(2):
        at = i * wide
        result = dot(inner, edn_v[:, at : at + wide])
        rhs[placed_at:theirs, at : at + wide] = (result * slot_gate).astype(BF16)
        send(
            rhs.at[pl.ds(placed_at, slots), pl.ds(at, wide)],
            rhs.at[pl.ds(theirs, slots), pl.ds(at, wide)],
            slot_sem.at[0], slot_sem.at[1 + i], partner,
        )

    wait_for(rhs.at[pl.ds(0, shared_units)], down_sem.at[1])
    wait_for(lhs.at[pl.ds(0, shared_units)], act_sem.at[1])
    chosen_half = (
        lax.broadcasted_iota(jnp.int32, (HALF, TOKENS), 1)
        == lax.broadcasted_iota(jnp.int32, (HALF, TOKENS), 0) + core * HALF
    ).astype(BF16)
    left = dot_nt(chosen_half, lhs[...]).astype(BF16)
    step = 256
    for i in range(2):
        wait_for(rhs.at[pl.ds(theirs, slots), pl.ds(i * wide, wide)], slot_sem.at[1 + i])
        for at in range(i * wide, (i + 1) * wide, step):
            part[:, at : at + step] = dot(left, rhs[:, at : at + step])
    for k in FAR_FIRST:
        rows = pl.ds(pl.multiple_of(((second + k) % RING) * RING, RING), RING)
        p_send[k - 1] = part[rows, :].astype(BF16)
        send(p_send.at[k - 1], p_recv.at[k - 1], p_sem.at[0], p_sem.at[1], on_second(k))
    summed = part[pl.ds(pl.multiple_of(second * RING, RING), RING), :]
    own_column = (
        lax.broadcasted_iota(jnp.int32, (HEADS, TOKENS), 1) == me
    ).astype(BF16)
    own = hid_tile + diagonal(dot_nt(own_column, proj_n[...]))
    wait_for(p_recv, p_sem.at[1])
    for k in range(RING - 1):
        summed = summed + p_recv[k].astype(F32)
    for h in range(HEADS):
        tok[pl.ds(h, RING, stride=HEADS), :] = summed[:, h * HEAD_DIM : (h + 1) * HEAD_DIM]
    for k in FAR_FIRST:
        to = pl.multiple_of(((first + k) % RING) * HEADS, HEADS)
        send(tok.at[pl.ds(to, HEADS)], t_recv.at[k - 1], t_sem.at[0], t_sem.at[1], on_first(k))
    own = own + tok[pl.ds(pl.multiple_of(first * HEADS, HEADS), HEADS), :]
    wait_for(t_recv, t_sem.at[1])
    for k in range(RING - 1):
        own = own + t_recv[k]
    for h in range(HEADS):
        out_ref[:, h * HEAD_DIM : (h + 1) * HEAD_DIM] = own[h : h + 1, :].astype(BF16)
    every_tile = pl.ds(0, TOKENS - 1)
    for buf, sem in ((att, att_sem), (hid, hid_sem), (pro, pro_sem)):
        wait_for(buf.at[every_tile], sem.at[0])
    wait_for(rhs.at[pl.ds(0, shared_units)], down_sem.at[0])
    wait_for(lhs.at[pl.ds(0, shared_units)], act_sem.at[0])
    wait_for(rhs.at[pl.ds(placed_at, slots)], slot_sem.at[0])
    wait_for(p_send, p_sem.at[0])
    wait_for(t_recv, t_sem.at[0])


def body(
    query, key_new, value_new, key_cache, value_cache, lengths, hidden, routes, w_out, ln_gain,
    router, shared_up, shared_down, expert_up, expert_down,
):
    key_cache = key_cache.reshape(key_cache.shape[1:])
    value_cache = value_cache.reshape(value_cache.shape[1:])
    lengths = lengths.reshape(1, 1)
    routes = routes.reshape(1, -1)
    ln_gain = ln_gain.reshape(-1, HEAD_DIM)
    w_out, router, shared_up = w_out.T, router.T, shared_up.T
    args = (
        query, key_new, value_new, key_cache, value_cache, lengths, hidden, routes, w_out, ln_gain,
        router, shared_up, shared_down, expert_up, expert_down,
    )
    d = query.shape[1]
    units = shared_up.shape[0]
    slots = TOKENS * 4 // 32
    tile = (TOKENS, HEADS, HEAD_DIM)

    def own(a):
        return pltpu.VMEM(a.shape, a.dtype)

    dma = pltpu.SemaphoreType.DMA
    scratch = [
        pltpu.VMEM((4, 1, d), BF16),
        own(key_cache),
        own(value_cache),
        own(lengths),
        own(routes),
        own(w_out),
        own(ln_gain),
        pltpu.VMEM((units + router.shape[0], d), BF16),
        pltpu.VMEM((2 * (units + slots), d), BF16),
        own(expert_up),
        own(expert_down),
        pltpu.VMEM(tile, BF16),
        pltpu.VMEM(tile, BF16),
        pltpu.VMEM((TOKENS, w_out.shape[0], TOKENS), BF16),
        pltpu.VMEM((TOKENS * HEADS, HEAD_DIM), F32),
        pltpu.VMEM((d, TOKENS), F32),
        pltpu.VMEM((d, TOKENS), F32),
        pltpu.VMEM((TOKENS, d), BF16),
        pltpu.VMEM((d, TOKENS), F32),
        pltpu.VMEM((d, TOKENS), BF16),
        pltpu.VMEM((d, TOKENS), BF16),
        pltpu.VMEM((HALF, d), F32),
        pltpu.VMEM((RING - 1, RING, d), BF16),
        pltpu.VMEM((RING - 1, RING, d), BF16),
        pltpu.VMEM((RING * HEADS, HEAD_DIM), F32),
        pltpu.VMEM((RING - 1, HEADS, HEAD_DIM), F32),
        pltpu.VMEM((2 * (units + slots), TOKENS), BF16),
    ]
    scratch += [dma((n,)) for n in (11, 16, 4, 16, 2, 2, 3, 2, 2)]
    return pl.pallas_call(
        kernel,
        out_shape=jax.ShapeDtypeStruct((1, d), BF16),
        in_specs=[pl.BlockSpec(memory_space=pl.ANY)] * 15,
        out_specs=pl.BlockSpec(memory_space=pltpu.VMEM),
        scratch_shapes=scratch,
        compiler_params=pltpu.CompilerParams(collective_id=0, has_side_effects=True),
        name="decode_layer",
    )(*args)


def solution(mesh):
    torus = Mesh(
        mesh.devices.reshape(mesh.shape["group"], RING, RING, 2),
        ("group", "expert_0", "expert_1", "expert_2"),
    )
    placed = (
        P(GROUP_EXPERT, None),
        P(GROUP_EXPERT, None),
        P(GROUP_EXPERT, None),
        P(GROUP_EXPERT, None, None),
        P(GROUP_EXPERT, None, None),
        P(GROUP_EXPERT),
        P(GROUP_EXPERT, None),
        P("group"),
        P(None, EXPERT),
        P(),
        P(),
        P(None, EXPERT),
        P(EXPERT, None),
        P(None, EXPERT),
        P(EXPERT, None),
    )
    return jax.shard_map(
        body, mesh=torus, in_specs=placed, out_specs=P(GROUP_EXPERT, None), check_vma=False
    )
```

time: 65.7 us -> 60 us (0.913)
  Pallas kernels: 63.6 us -> 57.9 us
    pallas_call x1, Pallas kernels: 63.6 us -> 57.9 us  [body(): pl.pallas_call(kernel, out_shape=jax.ShapeDtypeStruct((1, d), BF16), in_s...]
where the time goes in v4:
time: 60 us; the launch traced here: 59.8 us
  Pallas kernels  57.9 us (96%)
  local copies, waits for them, and re-layouts  1.3 us (2%)
  between operations  0.66 us (1%)
    pallas_call x1, Pallas kernels, body(): pl.pallas_call(kernel, out_shape=jax.ShapeDtypeStruct((1, d), BF16), in_s...  57.9 us
    unnamed x1, local copies, waits for them, and re-layouts  1.3 us

profile of v4, /device:TPU:514, one launch (start us, length us, event | category | flops | bytes accessed | tf_op | source)
XLA Modules:
  0.0 59.8 jit_solution(12585998822944477289)
XLA Ops:
  0.7 57.9 %decode_layer.1 = bf16[1,2048]{1,0:T(2,128)(2,1)} custom-call(bf16[1,2048]{1,0:T(2,128)(2,1)} %refs_0_.1, bf16[1,2048]{1,0:T(2,128)(2,1)} %refs_1_.1, bf16[1,2048]{1,0:T(2,128)(2,1)} %refs_2_.1, bf16[256,2048]{1,0:T(8,128)(2,1)} %bitcast.9, bf16[256,2048]{1,0:T(8,128)(2,1)} %bitcast.10, s32[1,1]{1,0:T(1,128)} %bitcast.8.refs_5_, bf16[1,2048]{1,0:T(2,128)(2,1)} %refs_6_.1, ...), custom_call_target="tpu_custom_call" | custom-call | tf_op jit(solution)/shard_map/decode_layer/pallas_call | solution.py:429
  58.5 1.3 %copy.18 = bf16[1,2048]{1,0:T(2,128)(2,1)} copy(bf16[1,2048]{1,0:T(2,128)(2,1)} %decode_layer.1) | data formatting | bytes 8192

commit v5 on v4

--- a/solution.py
+++ b/solution.py
@@ -18,8 +18,10 @@
 EXPERT = ("expert_0", "expert_1", "expert_2")
 GROUP_EXPERT = ("group", "expert_0", "expert_1", "expert_2")
 MESH = pl.DeviceIdType.MESH
+QUARTERS = 4
 F32 = jnp.float32
 BF16 = jnp.bfloat16
+FAR = RING // 2
 FAR_FIRST = (4, 3, 5, 2, 6, 1, 7)
 NEAR_FIRST = (1, 7, 2, 6, 3, 5, 4)
 
@@ -50,7 +52,8 @@
     ins, out_ref, vm, sems = refs[:15], refs[15], refs[16:-9], refs[-9:]
     (
         rows_v, k_v, v_v, len_v, rt_v, wo_t, gain_v, up_t, rhs, eup_v, edn_v, att, hid, pro, big,
-        hid_t, gain_b, nat, res, proj_n, norm_t, part, p_send, p_recv, tok, t_recv, lhs,
+        hid_t, gain_b, nat, res, proj_n, norm_t, p_send, p_recv, tok, t_send, t_recv,
+        lhs,
     ) = vm
     load_sem, att_sem, hid_sem, pro_sem, down_sem, act_sem, slot_sem, p_sem, t_sem = sems
     d_model = rows_v.shape[2]
@@ -64,18 +67,18 @@
     second = y * (1 - core) + x * core
     me = core * HALF + second * RING + first
 
-    def on_first(k):
+    def on_first(k, to=core):
         return {
             "expert_0": (x + k * (1 - core)) % RING,
             "expert_1": (y + k * core) % RING,
-            "expert_2": core,
+            "expert_2": to,
         }
 
-    def on_second(k):
+    def on_second(k, to=core):
         return {
             "expert_0": (x + k * core) % RING,
             "expert_1": (y + k * (1 - core)) % RING,
-            "expert_2": core,
+            "expert_2": to,
         }
 
     partner = {"expert_0": x, "expert_1": y, "expert_2": 1 - core}
@@ -85,6 +88,8 @@
         pl.semaphore_signal(barrier, inc=1, device_id=on_first(k), device_id_type=MESH)
         pl.semaphore_signal(barrier, inc=1, device_id=on_second(k), device_id_type=MESH)
     pl.semaphore_signal(barrier, inc=1, device_id=partner, device_id_type=MESH)
+    across = on_first(FAR, 1 - core)
+    pl.semaphore_signal(barrier, inc=1, device_id=across, device_id_type=MESH)
 
     query_v, key_v, value_v, hid_v = (rows_v.at[i] for i in range(4))
 
@@ -127,6 +132,7 @@
 
     def pass_on(buf, sem, k):
         tile = buf.at[pl.ds(slot_of(k), 1)]
+        send(tile, tile, sem.at[0], sem.at[16], on_second(FAR, 1 - core))
         for j in FAR_FIRST:
             send(tile, tile, sem.at[0], sem.at[8 + j], on_second(j))
 
@@ -147,10 +153,12 @@
         for j in NEAR_FIRST:
             row = buf.at[row_of(j)]
             wait_for(row, sem.at[8 + j])
-            send(row, row, sem.at[0], sem.at[1], partner)
+            if j != FAR:
+                send(row, row, sem.at[0], sem.at[1], partner)
 
     def tiles_4(buf, sem):
-        wait_for(buf.at[pl.ds((1 - core) * HALF, HALF)], sem.at[1])
+        wait_for(buf.at[pl.ds((1 - core) * HALF, HALF - RING)], sem.at[1])
+        wait_for(buf.at[pl.ds((1 - core) * HALF, RING)], sem.at[16])
 
     def steps_1(buf, sem):
         tile = buf.at[pl.ds(me, 1)]
@@ -200,7 +208,7 @@
     mixed = dot(weights, v_v[...]) + own_weight * spread(value_v)
     att[pl.ds(me, 1)] = diagonal(mixed).astype(BF16)[None]
 
-    pl.semaphore_wait(barrier, 2 * (RING - 1) + 1)
+    pl.semaphore_wait(barrier, 2 * RING)
     tiles_1(att, att_sem)
     steps_1(hid, hid_sem)
 
@@ -316,9 +324,9 @@
     eup_load.wait()
     inner = jax.nn.gelu(dot(picked, eup_v[...]), approximate=True).astype(BF16)
     edn_load.wait()
-    wide = d_model // 2
+    wide = d_model // QUARTERS
     theirs = placed_at + slots
-    for i in range(2):
+    for i in range(QUARTERS):
         at = i * wide
         result = dot(inner, edn_v[:, at : at + wide])
         rhs[placed_at:theirs, at : at + wide] = (result * slot_gate).astype(BF16)
@@ -335,16 +343,16 @@
         == lax.broadcasted_iota(jnp.int32, (HALF, TOKENS), 0) + core * HALF
     ).astype(BF16)
     left = dot_nt(chosen_half, lhs[...]).astype(BF16)
-    step = 256
-    for i in range(2):
-        wait_for(rhs.at[pl.ds(theirs, slots), pl.ds(i * wide, wide)], slot_sem.at[1 + i])
-        for at in range(i * wide, (i + 1) * wide, step):
-            part[:, at : at + step] = dot(left, rhs[:, at : at + step])
-    for k in FAR_FIRST:
-        rows = pl.ds(pl.multiple_of(((second + k) % RING) * RING, RING), RING)
-        p_send[k - 1] = part[rows, :].astype(BF16)
-        send(p_send.at[k - 1], p_recv.at[k - 1], p_sem.at[0], p_sem.at[1], on_second(k))
-    summed = part[pl.ds(pl.multiple_of(second * RING, RING), RING), :]
+    for i in range(QUARTERS):
+        columns = pl.ds(i * wide, wide)
+        wait_for(rhs.at[pl.ds(theirs, slots), columns], slot_sem.at[1 + i])
+        for at in range(i * wide, (i + 1) * wide, 256):
+            piece = dot(left, rhs[:, at : at + 256]).astype(BF16)
+            p_send[:, :, at : at + 256] = piece.reshape(RING, RING, 256)
+        for k in FAR_FIRST:
+            block = p_send.at[(second + k) % RING, :, columns]
+            send(block, p_recv.at[k - 1, :, columns], p_sem.at[0], p_sem.at[1], on_second(k))
+    summed = p_send[second].astype(F32)
     own_column = (
         lax.broadcasted_iota(jnp.int32, (HEADS, TOKENS), 1) == me
     ).astype(BF16)
@@ -354,13 +362,14 @@
         summed = summed + p_recv[k].astype(F32)
     for h in range(HEADS):
         tok[pl.ds(h, RING, stride=HEADS), :] = summed[:, h * HEAD_DIM : (h + 1) * HEAD_DIM]
+    t_send[...] = tok[...].astype(BF16)
     for k in FAR_FIRST:
         to = pl.multiple_of(((first + k) % RING) * HEADS, HEADS)
-        send(tok.at[pl.ds(to, HEADS)], t_recv.at[k - 1], t_sem.at[0], t_sem.at[1], on_first(k))
+        send(t_send.at[pl.ds(to, HEADS)], t_recv.at[k - 1], t_sem.at[0], t_sem.at[1], on_first(k))
     own = own + tok[pl.ds(pl.multiple_of(first * HEADS, HEADS), HEADS), :]
     wait_for(t_recv, t_sem.at[1])
     for k in range(RING - 1):
-        own = own + t_recv[k]
+        own = own + t_recv[k].astype(F32)
     for h in range(HEADS):
         out_ref[:, h * HEAD_DIM : (h + 1) * HEAD_DIM] = own[h : h + 1, :].astype(BF16)
     every_tile = pl.ds(0, TOKENS - 1)
@@ -369,7 +378,7 @@
     wait_for(rhs.at[pl.ds(0, shared_units)], down_sem.at[0])
     wait_for(lhs.at[pl.ds(0, shared_units)], act_sem.at[0])
     wait_for(rhs.at[pl.ds(placed_at, slots)], slot_sem.at[0])
-    wait_for(p_send, p_sem.at[0])
+    wait_for(p_recv, p_sem.at[0])
     wait_for(t_recv, t_sem.at[0])
 
 
@@ -418,14 +427,14 @@
         pltpu.VMEM((d, TOKENS), F32),
         pltpu.VMEM((d, TOKENS), BF16),
         pltpu.VMEM((d, TOKENS), BF16),
-        pltpu.VMEM((HALF, d), F32),
-        pltpu.VMEM((RING - 1, RING, d), BF16),
+        pltpu.VMEM((RING, RING, d), BF16),
         pltpu.VMEM((RING - 1, RING, d), BF16),
         pltpu.VMEM((RING * HEADS, HEAD_DIM), F32),
-        pltpu.VMEM((RING - 1, HEADS, HEAD_DIM), F32),
+        pltpu.VMEM((RING * HEADS, HEAD_DIM), BF16),
+        pltpu.VMEM((RING - 1, HEADS, HEAD_DIM), BF16),
         pltpu.VMEM((2 * (units + slots), TOKENS), BF16),
     ]
-    scratch += [dma((n,)) for n in (11, 16, 4, 16, 2, 2, 3, 2, 2)]
+    scratch += [dma((n,)) for n in (11, 17, 4, 17, 2, 2, 1 + QUARTERS, 2, 2)]
     return pl.pallas_call(
         kernel,
         out_shape=jax.ShapeDtypeStruct((1, d), BF16),

time: 60 us -> 61.1 us (1.018)
  Pallas kernels: 57.9 us -> 58.6 us
    pallas_call x1, Pallas kernels: 57.9 us -> 58.6 us  [body(): pl.pallas_call(kernel, out_shape=jax.ShapeDtypeStruct((1, d), BF16), in_s...]
where the time goes in v5:
time: 61.1 us; the launch traced here: 60.6 us
  Pallas kernels  58.6 us (96%)
  local copies, waits for them, and re-layouts  1.3 us (2%)
  between operations  0.66 us (1%)
    pallas_call x1, Pallas kernels, body(): pl.pallas_call(kernel, out_shape=jax.ShapeDtypeStruct((1, d), BF16), in_s...  58.6 us
    unnamed x1, local copies, waits for them, and re-layouts  1.3 us

profile of v5, /device:TPU:514, one launch (start us, length us, event | category | flops | bytes accessed | tf_op | source)
XLA Modules:
  0.0 60.6 jit_solution(2985449694330549580)
XLA Ops:
  0.7 58.6 %decode_layer.1 = bf16[1,2048]{1,0:T(2,128)(2,1)} custom-call(bf16[1,2048]{1,0:T(2,128)(2,1)} %refs_0_.1, bf16[1,2048]{1,0:T(2,128)(2,1)} %refs_1_.1, bf16[1,2048]{1,0:T(2,128)(2,1)} %refs_2_.1, bf16[256,2048]{1,0:T(8,128)(2,1)} %bitcast.9, bf16[256,2048]{1,0:T(8,128)(2,1)} %bitcast.10, s32[1,1]{1,0:T(1,128)} %bitcast.8.refs_5_, bf16[1,2048]{1,0:T(2,128)(2,1)} %refs_6_.1, ...), custom_call_target="tpu_custom_call" | custom-call | tf_op jit(solution)/shard_map/decode_layer/pallas_call | solution.py:438
  59.2 1.3 %copy.18 = bf16[1,2048]{1,0:T(2,128)(2,1)} copy(bf16[1,2048]{1,0:T(2,128)(2,1)} %decode_layer.1) | data formatting | bytes 8192

commit v6 on v4

--- a/solution.py
+++ b/solution.py
@@ -18,6 +18,7 @@
 EXPERT = ("expert_0", "expert_1", "expert_2")
 GROUP_EXPERT = ("group", "expert_0", "expert_1", "expert_2")
 MESH = pl.DeviceIdType.MESH
+PIECES = 2
 F32 = jnp.float32
 BF16 = jnp.bfloat16
 FAR_FIRST = (4, 3, 5, 2, 6, 1, 7)
@@ -50,9 +51,9 @@
     ins, out_ref, vm, sems = refs[:15], refs[15], refs[16:-9], refs[-9:]
     (
         rows_v, k_v, v_v, len_v, rt_v, wo_t, gain_v, up_t, rhs, eup_v, edn_v, att, hid, pro, big,
-        hid_t, gain_b, nat, res, proj_n, norm_t, part, p_send, p_recv, tok, t_recv, lhs,
+        hid_t, gain_b, nat, res, proj_n, norm_t, p_send, p_recv, tok, t_recv, lhs,
     ) = vm
-    load_sem, att_sem, hid_sem, pro_sem, down_sem, act_sem, slot_sem, p_sem, t_sem = sems
+    load_sem, att_sem, hid_sem, pro_sem, down_sem, up_sem, slot_sem, p_sem, t_sem = sems
     d_model = rows_v.shape[2]
     experts, shared_units = ins[10].shape[0], ins[11].shape[0]
     slots = TOKENS * 4 // 32
@@ -81,7 +82,7 @@
     partner = {"expert_0": x, "expert_1": y, "expert_2": 1 - core}
 
     barrier = pltpu.get_barrier_semaphore()
-    for k in range(1, RING):
+    for k in FAR_FIRST:
         pl.semaphore_signal(barrier, inc=1, device_id=on_first(k), device_id_type=MESH)
         pl.semaphore_signal(barrier, inc=1, device_id=on_second(k), device_id_type=MESH)
     pl.semaphore_signal(barrier, inc=1, device_id=partner, device_id_type=MESH)
@@ -104,8 +105,11 @@
     down_load = load(12, rhs.at[pl.ds(0, shared_units)], 6)
     wo_load = load(8, wo_t, 7)
     load(11, up_t.at[pl.ds(0, shared_units)], 8)
-    load(10, up_t.at[pl.ds(shared_units, experts)], 8)
-    up_load = pltpu.make_async_copy(up_t, up_t, load_sem.at[8])
+    load(10, up_t.at[pl.ds(2 * shared_units, experts)], 8)
+    up_load = pltpu.make_async_copy(
+        up_t.at[pl.ds(0, shared_units + experts)], up_t.at[pl.ds(0, shared_units + experts)],
+        load_sem.at[8],
+    )
     eup_load = load(13, eup_v, 9)
     edn_load = load(14, edn_v, 10)
 
@@ -130,21 +134,26 @@
         for j in FAR_FIRST:
             send(tile, tile, sem.at[0], sem.at[8 + j], on_second(j))
 
+    def zero_last(at):
+        last = NEAR_FIRST[-1]
+        order = [k + (last - k) * (1 - ((k - at + RING) % RING + RING - 1) // RING) for k in NEAR_FIRST[:-1]]
+        return order + [at + last * (1 - (at + RING - 1) // RING)]
+
     def tiles_1(buf, sem):
         tile = buf.at[pl.ds(me, 1)]
         for k in FAR_FIRST:
             send(tile, tile, sem.at[0], sem.at[1 + k], on_first(k))
         pass_on(buf, sem, 0)
 
-    def tiles_2(buf, sem):
-        for k in NEAR_FIRST:
+    def tiles_2(buf, sem, order):
+        for k in order:
             wait_for(buf.at[pl.ds(slot_of(k), 1)], sem.at[1 + k])
             pass_on(buf, sem, k)
         row = buf.at[row_of(0)]
         send(row, row, sem.at[0], sem.at[1], partner)
 
-    def tiles_3(buf, sem):
-        for j in NEAR_FIRST:
+    def tiles_3(buf, sem, order):
+        for j in order:
             row = buf.at[row_of(j)]
             wait_for(row, sem.at[8 + j])
             send(row, row, sem.at[0], sem.at[1], partner)
@@ -241,37 +250,43 @@
         rhs.at[pl.ds(0, shared_units)], rhs.at[pl.ds(shared_units, shared_units)], down_sem.at[0],
         down_sem.at[1], partner,
     )
-
-    tiles_2(att, att_sem)
-    tiles_3(att, att_sem)
+    up_load.wait()
+    send(
+        up_t.at[pl.ds(0, shared_units)], up_t.at[pl.ds(shared_units, shared_units)], up_sem.at[0],
+        up_sem.at[1], partner,
+    )
+
+    tiles_2(att, att_sem, zero_last(first))
+    tiles_3(att, att_sem, zero_last(second))
     steps_2(hid, hid_sem)
 
-    def relayout(buf, at):
+    def projected(at):
         at = pl.multiple_of(at, HALF)
-        rows = pl.ds(pl.multiple_of(at * HEADS, HALF * HEADS), HALF * HEADS)
-        big[rows, :] = buf[pl.ds(at, HALF)].reshape(HALF * HEADS, HEAD_DIM).astype(F32)
-
-    def att_rows(at):
-        relayout(att, at)
-        at = pl.multiple_of(at, HALF)
+        every = pl.ds(pl.multiple_of(at * HEADS, HALF * HEADS), HALF * HEADS)
+        big[every, :] = att[pl.ds(at, HALF)].reshape(HALF * HEADS, HEAD_DIM).astype(F32)
         for h in range(HEADS):
-            nat[pl.ds(at, HALF), h * HEAD_DIM : (h + 1) * HEAD_DIM] = big[
+            nat[:, h * HEAD_DIM : (h + 1) * HEAD_DIM] = big[
                 pl.ds(at * HEADS + h, HALF, stride=HEADS), :
             ].astype(BF16)
-
-    att_rows(core * HALF)
+        return dot_nt(wo_t[...], nat[...])
+
+    wo_load.wait()
+    here = projected(core * HALF)
     tiles_4(att, att_sem)
-    att_rows((1 - core) * HALF)
-    wo_load.wait()
-    pro[pl.ds(me, 1)] = dot_nt(wo_t[...], nat[...]).astype(BF16)[None]
+    there = projected((1 - core) * HALF)
+    pro[me] = jnp.where(
+        core == 0,
+        jnp.concatenate([here, there], axis=1),
+        jnp.concatenate([there, here], axis=1),
+    ).astype(BF16)
     tiles_1(pro, pro_sem)
-    tiles_2(pro, pro_sem)
+    tiles_2(pro, pro_sem, NEAR_FIRST)
     steps_3(hid, hid_sem)
     steps_4(hid, hid_sem)
     big[...] = hid[...].reshape(TOKENS * HEADS, HEAD_DIM).astype(F32)
     for h in range(HEADS):
         hid_t[h * HEAD_DIM : (h + 1) * HEAD_DIM, :] = big[pl.ds(h, TOKENS, stride=HEADS), :].T
-    tiles_3(pro, pro_sem)
+    tiles_3(pro, pro_sem, NEAR_FIRST)
     tiles_4(pro, pro_sem)
 
     cols = wo_t.shape[0]
@@ -296,18 +311,12 @@
         rows = slice(h * HEAD_DIM, (h + 1) * HEAD_DIM)
         norm_t[rows, :] = ((res[rows, :] - mean) * inverse * gain_b[rows, :]).astype(BF16)
 
-    up_load.wait()
     normed = norm_t[...]
-    both = dot(up_t[...], normed)
-    lhs[0:shared_units, :] = jax.nn.gelu(both[0:shared_units], approximate=True).astype(BF16)
-    send(
-        lhs.at[pl.ds(0, shared_units)], lhs.at[pl.ds(shared_units, shared_units)], act_sem.at[0],
-        act_sem.at[1], partner,
-    )
     picked = dot_nt(placed.astype(BF16), normed).astype(BF16)
+    logits = dot(up_t[2 * shared_units :, :], normed)
     expert_row = lax.broadcasted_iota(jnp.int32, (experts, TOKENS), 0)
     chosen = jnp.sum(
-        jnp.where(jnp.broadcast_to(routes, (experts, TOKENS)) == expert_row, both[shared_units:], 0.0),
+        jnp.where(jnp.broadcast_to(routes, (experts, TOKENS)) == expert_row, logits, 0.0),
         axis=0,
         keepdims=True,
     )
@@ -316,9 +325,9 @@
     eup_load.wait()
     inner = jax.nn.gelu(dot(picked, eup_v[...]), approximate=True).astype(BF16)
     edn_load.wait()
-    wide = d_model // 2
+    wide = d_model // PIECES
     theirs = placed_at + slots
-    for i in range(2):
+    for i in range(PIECES):
         at = i * wide
         result = dot(inner, edn_v[:, at : at + wide])
         rhs[placed_at:theirs, at : at + wide] = (result * slot_gate).astype(BF16)
@@ -329,22 +338,24 @@
         )
 
     wait_for(rhs.at[pl.ds(0, shared_units)], down_sem.at[1])
-    wait_for(lhs.at[pl.ds(0, shared_units)], act_sem.at[1])
+    wait_for(up_t.at[pl.ds(0, shared_units)], up_sem.at[1])
+    both = dot(up_t[0 : 2 * shared_units, :], normed)
+    lhs[0 : 2 * shared_units, :] = jax.nn.gelu(both, approximate=True).astype(BF16)
     chosen_half = (
         lax.broadcasted_iota(jnp.int32, (HALF, TOKENS), 1)
         == lax.broadcasted_iota(jnp.int32, (HALF, TOKENS), 0) + core * HALF
     ).astype(BF16)
     left = dot_nt(chosen_half, lhs[...]).astype(BF16)
-    step = 256
-    for i in range(2):
-        wait_for(rhs.at[pl.ds(theirs, slots), pl.ds(i * wide, wide)], slot_sem.at[1 + i])
-        for at in range(i * wide, (i + 1) * wide, step):
-            part[:, at : at + step] = dot(left, rhs[:, at : at + step])
-    for k in FAR_FIRST:
-        rows = pl.ds(pl.multiple_of(((second + k) % RING) * RING, RING), RING)
-        p_send[k - 1] = part[rows, :].astype(BF16)
-        send(p_send.at[k - 1], p_recv.at[k - 1], p_sem.at[0], p_sem.at[1], on_second(k))
-    summed = part[pl.ds(pl.multiple_of(second * RING, RING), RING), :]
+    for i in range(PIECES):
+        columns = pl.ds(i * wide, wide)
+        wait_for(rhs.at[pl.ds(theirs, slots), columns], slot_sem.at[1 + i])
+        for at in range(i * wide, (i + 1) * wide, 256):
+            piece = dot(left, rhs[:, at : at + 256]).astype(BF16)
+            p_send[:, :, at : at + 256] = piece.reshape(RING, RING, 256)
+        for k in FAR_FIRST:
+            block = p_send.at[(second + k) % RING, :, columns]
+            send(block, p_recv.at[k - 1, :, columns], p_sem.at[0], p_sem.at[1], on_second(k))
+    summed = p_send[second].astype(F32)
     own_column = (
         lax.broadcasted_iota(jnp.int32, (HEADS, TOKENS), 1) == me
     ).astype(BF16)
@@ -367,9 +378,9 @@
     for buf, sem in ((att, att_sem), (hid, hid_sem), (pro, pro_sem)):
         wait_for(buf.at[every_tile], sem.at[0])
     wait_for(rhs.at[pl.ds(0, shared_units)], down_sem.at[0])
-    wait_for(lhs.at[pl.ds(0, shared_units)], act_sem.at[0])
+    wait_for(up_t.at[pl.ds(0, shared_units)], up_sem.at[0])
     wait_for(rhs.at[pl.ds(placed_at, slots)], slot_sem.at[0])
-    wait_for(p_send, p_sem.at[0])
+    wait_for(p_recv, p_sem.at[0])
     wait_for(t_recv, t_sem.at[0])
 
 
@@ -404,7 +415,7 @@
         own(routes),
         own(w_out),
         own(ln_gain),
-        pltpu.VMEM((units + router.shape[0], d), BF16),
+        pltpu.VMEM((2 * units + router.shape[0], d), BF16),
         pltpu.VMEM((2 * (units + slots), d), BF16),
         own(expert_up),
         own(expert_down),
@@ -414,18 +425,17 @@
         pltpu.VMEM((TOKENS * HEADS, HEAD_DIM), F32),
         pltpu.VMEM((d, TOKENS), F32),
         pltpu.VMEM((d, TOKENS), F32),
-        pltpu.VMEM((TOKENS, d), BF16),
+        pltpu.VMEM((HALF, d), BF16),
         pltpu.VMEM((d, TOKENS), F32),
         pltpu.VMEM((d, TOKENS), BF16),
         pltpu.VMEM((d, TOKENS), BF16),
-        pltpu.VMEM((HALF, d), F32),
-        pltpu.VMEM((RING - 1, RING, d), BF16),
+        pltpu.VMEM((RING, RING, d), BF16),
         pltpu.VMEM((RING - 1, RING, d), BF16),
         pltpu.VMEM((RING * HEADS, HEAD_DIM), F32),
         pltpu.VMEM((RING - 1, HEADS, HEAD_DIM), F32),
         pltpu.VMEM((2 * (units + slots), TOKENS), BF16),
     ]
-    scratch += [dma((n,)) for n in (11, 16, 4, 16, 2, 2, 3, 2, 2)]
+    scratch += [dma((n,)) for n in (11, 16, 4, 16, 2, 2, 1 + PIECES, 2, 2)]
     return pl.pallas_call(
         kernel,
         out_shape=jax.ShapeDtypeStruct((1, d), BF16),

time: 60 us -> 59.1 us (0.985)
  Pallas kernels: 57.9 us -> 57 us
    pallas_call x1, Pallas kernels: 57.9 us -> 57 us  [body(): pl.pallas_call(kernel, out_shape=jax.ShapeDtypeStruct((1, d), BF16), in_s...]
where the time goes in v6:
time: 59.1 us; the launch traced here: 58.9 us
  Pallas kernels  57 us (96%)
  local copies, waits for them, and re-layouts  1.3 us (2%)
  between operations  0.66 us (1%)
    pallas_call x1, Pallas kernels, body(): pl.pallas_call(kernel, out_shape=jax.ShapeDtypeStruct((1, d), BF16), in_s...  57 us
    unnamed x1, local copies, waits for them, and re-layouts  1.3 us

profile of v6, /device:TPU:514, one launch (start us, length us, event | category | flops | bytes accessed | tf_op | source)
XLA Modules:
  0.0 58.9 jit_solution(1990099075685898759)
XLA Ops:
  0.7 57.0 %decode_layer.1 = bf16[1,2048]{1,0:T(2,128)(2,1)} custom-call(bf16[1,2048]{1,0:T(2,128)(2,1)} %refs_0_.1, bf16[1,2048]{1,0:T(2,128)(2,1)} %refs_1_.1, bf16[1,2048]{1,0:T(2,128)(2,1)} %refs_2_.1, bf16[256,2048]{1,0:T(8,128)(2,1)} %bitcast.9, bf16[256,2048]{1,0:T(8,128)(2,1)} %bitcast.10, s32[1,1]{1,0:T(1,128)} %bitcast.8.refs_5_, bf16[1,2048]{1,0:T(2,128)(2,1)} %refs_6_.1, ...), custom_call_target="tpu_custom_call" | custom-call | tf_op jit(solution)/shard_map/decode_layer/pallas_call | solution.py:439
  57.6 1.3 %copy.18 = bf16[1,2048]{1,0:T(2,128)(2,1)} copy(bf16[1,2048]{1,0:T(2,128)(2,1)} %decode_layer.1) | data formatting | bytes 8192

commit v7 on v6

--- a/solution.py
+++ b/solution.py
@@ -19,8 +19,11 @@
 GROUP_EXPERT = ("group", "expert_0", "expert_1", "expert_2")
 MESH = pl.DeviceIdType.MESH
 PIECES = 2
+KEPT = 2
 F32 = jnp.float32
 BF16 = jnp.bfloat16
+OWN = 0
+PAIRS = ((1, 7), (2, 6), (3, 5), (4,))
 FAR_FIRST = (4, 3, 5, 2, 6, 1, 7)
 NEAR_FIRST = (1, 7, 2, 6, 3, 5, 4)
 
@@ -48,12 +51,12 @@
 
 
 def kernel(*refs):
-    ins, out_ref, vm, sems = refs[:15], refs[15], refs[16:-9], refs[-9:]
+    ins, out_ref, vm, sems = refs[:15], refs[15], refs[16:-10], refs[-10:]
     (
         rows_v, k_v, v_v, len_v, rt_v, wo_t, gain_v, up_t, rhs, eup_v, edn_v, att, hid, pro, big,
         hid_t, gain_b, nat, res, proj_n, norm_t, p_send, p_recv, tok, t_recv, lhs,
     ) = vm
-    load_sem, att_sem, hid_sem, pro_sem, down_sem, up_sem, slot_sem, p_sem, t_sem = sems
+    load_sem, att_sem, hid_sem, pro_sem, down_sem, up_sem, slot_sem, p_sem, t_sem, units_sem = sems
     d_model = rows_v.shape[2]
     experts, shared_units = ins[10].shape[0], ins[11].shape[0]
     slots = TOKENS * 4 // 32
@@ -79,6 +82,13 @@
             "expert_2": core,
         }
 
+    def along(axis, k, to):
+        return {
+            "expert_0": (x + k * (1 - axis)) % RING,
+            "expert_1": (y + k * axis) % RING,
+            "expert_2": to,
+        }
+
     partner = {"expert_0": x, "expert_1": y, "expert_2": 1 - core}
 
     barrier = pltpu.get_barrier_semaphore()
@@ -86,6 +96,12 @@
         pl.semaphore_signal(barrier, inc=1, device_id=on_first(k), device_id_type=MESH)
         pl.semaphore_signal(barrier, inc=1, device_id=on_second(k), device_id_type=MESH)
     pl.semaphore_signal(barrier, inc=1, device_id=partner, device_id_type=MESH)
+
+    @pl.when(core == 1)
+    def _():
+        for k in FAR_FIRST:
+            pl.semaphore_signal(barrier, inc=1, device_id=along(0, k, 0), device_id_type=MESH)
+
 
     query_v, key_v, value_v, hid_v = (rows_v.at[i] for i in range(4))
 
@@ -110,8 +126,11 @@
         up_t.at[pl.ds(0, shared_units + experts)], up_t.at[pl.ds(0, shared_units + experts)],
         load_sem.at[8],
     )
-    eup_load = load(13, eup_v, 9)
-    edn_load = load(14, edn_v, 10)
+    units = ins[13].shape[1]
+    kept = units // KEPT
+    moved = units - kept
+    eup_load = load(13, eup_v.at[:, pl.ds(0, units)], 9)
+    edn_load = load(14, edn_v.at[pl.ds(0, units)], 10)
 
     def send(src, dst, send_sem, recv_sem, to):
         copy = pltpu.make_async_remote_copy(
@@ -123,43 +142,87 @@
     def wait_for(ref, sem):
         pltpu.make_async_copy(ref, ref, sem).wait()
 
-    def slot_of(k):
-        return core * HALF + second * RING + (first - k + RING) % RING
-
-    def row_of(second_k, of=core):
-        return pl.ds(of * HALF + ((second - second_k + RING) % RING) * RING, RING)
-
-    def pass_on(buf, sem, k):
-        tile = buf.at[pl.ds(slot_of(k), 1)]
+    def row_of(second_k):
+        return pl.ds(core * HALF + ((second - second_k + RING) % RING) * RING, RING)
+
+    place = ((x, y), (y, x))
+
+    def tile_at(buf, color, k):
+        at, row = place[color]
+        return buf.at[pl.ds(color * HALF + row * RING + (at - k + RING) % RING, 1)]
+
+    def row_at(buf, color, j):
+        return buf.at[
+            pl.ds(color * HALF + ((place[color][1] - j + RING) % RING) * RING, RING)
+        ]
+
+    def pass_on(buf, sem, color, k):
+        tile = tile_at(buf, color, k)
         for j in FAR_FIRST:
-            send(tile, tile, sem.at[0], sem.at[8 + j], on_second(j))
+            pair = 19 + 4 * color + min(j, RING - j) - 1
+            send(tile, tile, sem.at[1 - color], sem.at[pair], along(1 - color, j, 1))
+
+    def tiles_1(buf, sem):
+        tile = buf.at[pl.ds(me, 1)]
+
+        @pl.when(core == 0)
+        def _():
+            for k in FAR_FIRST:
+                send(tile, tile, sem.at[0], sem.at[4 + k], along(0, k, 1))
+            send(tile, tile, sem.at[0], sem.at[4], partner)
+
+        @pl.when(core == 1)
+        def _():
+            for k in FAR_FIRST:
+                send(tile, tile, sem.at[0], sem.at[11 + k], along(1, k, 1))
+            pass_on(buf, sem, 1, 0)
 
     def zero_last(at):
         last = NEAR_FIRST[-1]
-        order = [k + (last - k) * (1 - ((k - at + RING) % RING + RING - 1) // RING) for k in NEAR_FIRST[:-1]]
+        order = [
+            k + (last - k) * (1 - ((k - at + RING) % RING + RING - 1) // RING)
+            for k in NEAR_FIRST[:-1]
+        ]
         return order + [at + last * (1 - (at + RING - 1) // RING)]
 
-    def tiles_1(buf, sem):
-        tile = buf.at[pl.ds(me, 1)]
-        for k in FAR_FIRST:
-            send(tile, tile, sem.at[0], sem.at[1 + k], on_first(k))
-        pass_on(buf, sem, 0)
-
     def tiles_2(buf, sem, order):
-        for k in order:
-            wait_for(buf.at[pl.ds(slot_of(k), 1)], sem.at[1 + k])
-            pass_on(buf, sem, k)
-        row = buf.at[row_of(0)]
-        send(row, row, sem.at[0], sem.at[1], partner)
-
-    def tiles_3(buf, sem, order):
-        for j in order:
-            row = buf.at[row_of(j)]
-            wait_for(row, sem.at[8 + j])
-            send(row, row, sem.at[0], sem.at[1], partner)
-
-    def tiles_4(buf, sem):
-        wait_for(buf.at[pl.ds((1 - core) * HALF, HALF)], sem.at[1])
+        @pl.when(core == 1)
+        def _():
+            rows_left = RING - 1
+            for color, k in order:
+                tile = tile_at(buf, color, k)
+                wait_for(tile, sem.at[(4, 11)[color] + k])
+                pass_on(buf, sem, color, k)
+                if color:
+                    rows_left -= 1
+                    if not rows_left:
+                        row = row_at(buf, 1, 0)
+                        send(row, row, sem.at[0], sem.at[2], partner)
+                elif k is not OWN:
+                    send(tile, tile, sem.at[1], sem.at[3], partner)
+
+    def tiles_3(buf, sem, color):
+        @pl.when(core == 1)
+        def _():
+            for i, pair in enumerate(PAIRS):
+                wait_for(buf.at[pl.ds(0, RING * len(pair))], sem.at[19 + 4 * color + i])
+                for j in pair:
+                    row = row_at(buf, color, j)
+                    send(row, row, sem.at[1 - color], sem.at[3 - color], partner)
+
+        @pl.when(core == 0)
+        def _():
+            wait_for(buf.at[pl.ds(0, HALF - 1 + color)], sem.at[3 - color])
+
+    def tiles_sent(buf, sem):
+        @pl.when(core == 1)
+        def _():
+            wait_for(buf.at[pl.ds(0, 2 * HALF - 1)], sem.at[0])
+            wait_for(buf.at[pl.ds(0, 2 * HALF - RING - 1)], sem.at[1])
+
+        @pl.when(core == 0)
+        def _():
+            wait_for(buf.at[pl.ds(0, RING)], sem.at[0])
 
     def steps_1(buf, sem):
         tile = buf.at[pl.ds(me, 1)]
@@ -209,7 +272,7 @@
     mixed = dot(weights, v_v[...]) + own_weight * spread(value_v)
     att[pl.ds(me, 1)] = diagonal(mixed).astype(BF16)[None]
 
-    pl.semaphore_wait(barrier, 2 * (RING - 1) + 1)
+    pl.semaphore_wait(barrier, (2 + (1 - core)) * (RING - 1) + 1)
     tiles_1(att, att_sem)
     steps_1(hid, hid_sem)
 
@@ -230,7 +293,7 @@
         jnp.broadcast_to(rt_v[...], (8, TOKENS)).astype(F32).astype(BF16), to_slot
     )[0:1].astype(jnp.int32)
     device = (x * RING + y) * 2 + core
-    mine = device * eup_v.shape[1] // FF
+    mine = device * ins[13].shape[1] // FF
     member = routes == mine
     rank = dot(
         jnp.broadcast_to(member.astype(F32), (8, TOKENS)).astype(BF16), (nat_id <= lane).astype(BF16)
@@ -250,19 +313,35 @@
         rhs.at[pl.ds(0, shared_units)], rhs.at[pl.ds(shared_units, shared_units)], down_sem.at[0],
         down_sem.at[1], partner,
     )
+
+    @pl.when(core == 0)
+    def _():
+        eup_load.wait()
+        send(
+            eup_v.at[:, pl.ds(kept, moved)], eup_v.at[:, pl.ds(units, moved)], units_sem.at[0],
+            units_sem.at[1], partner,
+        )
+        edn_load.wait()
+        send(
+            edn_v.at[pl.ds(kept, moved)], edn_v.at[pl.ds(units, moved)], units_sem.at[2],
+            units_sem.at[3], partner,
+        )
+
     up_load.wait()
     send(
         up_t.at[pl.ds(0, shared_units)], up_t.at[pl.ds(shared_units, shared_units)], up_sem.at[0],
         up_sem.at[1], partner,
     )
 
-    tiles_2(att, att_sem, zero_last(first))
-    tiles_3(att, att_sem, zero_last(second))
-    steps_2(hid, hid_sem)
+    late_x = zero_last(x)
+    tiles_2(
+        att, att_sem,
+        [(1, k) for k in zero_last(y)] + [(0, k) for k in late_x[:-1] + [OWN] + late_x[-1:]],
+    )
+    tiles_3(att, att_sem, 1)
 
     def projected(at):
-        at = pl.multiple_of(at, HALF)
-        every = pl.ds(pl.multiple_of(at * HEADS, HALF * HEADS), HALF * HEADS)
+        every = pl.ds(at * HEADS, HALF * HEADS)
         big[every, :] = att[pl.ds(at, HALF)].reshape(HALF * HEADS, HEAD_DIM).astype(F32)
         for h in range(HEADS):
             nat[:, h * HEAD_DIM : (h + 1) * HEAD_DIM] = big[
@@ -271,23 +350,20 @@
         return dot_nt(wo_t[...], nat[...])
 
     wo_load.wait()
-    here = projected(core * HALF)
-    tiles_4(att, att_sem)
-    there = projected((1 - core) * HALF)
-    pro[me] = jnp.where(
-        core == 0,
-        jnp.concatenate([here, there], axis=1),
-        jnp.concatenate([there, here], axis=1),
-    ).astype(BF16)
+    half_1 = projected(HALF)
+    tiles_3(att, att_sem, 0)
+    steps_2(hid, hid_sem)
+    half_0 = projected(0)
+    pro[me] = jnp.concatenate([half_0, half_1], axis=1).astype(BF16)
     tiles_1(pro, pro_sem)
-    tiles_2(pro, pro_sem, NEAR_FIRST)
+    tiles_2(pro, pro_sem, [(0, OWN)] + [(color, k) for k in NEAR_FIRST for color in (1, 0)])
     steps_3(hid, hid_sem)
     steps_4(hid, hid_sem)
     big[...] = hid[...].reshape(TOKENS * HEADS, HEAD_DIM).astype(F32)
     for h in range(HEADS):
         hid_t[h * HEAD_DIM : (h + 1) * HEAD_DIM, :] = big[pl.ds(h, TOKENS, stride=HEADS), :].T
-    tiles_3(pro, pro_sem, NEAR_FIRST)
-    tiles_4(pro, pro_sem)
+    tiles_3(pro, pro_sem, 1)
+    tiles_3(pro, pro_sem, 0)
 
     cols = wo_t.shape[0]
     total = jnp.zeros((cols, TOKENS), F32)
@@ -322,20 +398,32 @@
     )
     gate = 1.0 / (1.0 + jnp.exp(-chosen))
     slot_gate = jnp.sum(placed * gate, axis=1, keepdims=True)
-    eup_load.wait()
-    inner = jax.nn.gelu(dot(picked, eup_v[...]), approximate=True).astype(BF16)
-    edn_load.wait()
     wide = d_model // PIECES
     theirs = placed_at + slots
-    for i in range(PIECES):
-        at = i * wide
-        result = dot(inner, edn_v[:, at : at + wide])
-        rhs[placed_at:theirs, at : at + wide] = (result * slot_gate).astype(BF16)
-        send(
-            rhs.at[pl.ds(placed_at, slots), pl.ds(at, wide)],
-            rhs.at[pl.ds(theirs, slots), pl.ds(at, wide)],
-            slot_sem.at[0], slot_sem.at[1 + i], partner,
-        )
+
+    def expert(count):
+        inner = jax.nn.gelu(dot(picked, eup_v[:, 0:count]), approximate=True).astype(BF16)
+        for i in range(PIECES):
+            at = i * wide
+            result = dot(inner, edn_v[0:count, at : at + wide])
+            rhs[placed_at:theirs, at : at + wide] = (result * slot_gate).astype(BF16)
+            send(
+                rhs.at[pl.ds(placed_at, slots), pl.ds(at, wide)],
+                rhs.at[pl.ds(theirs, slots), pl.ds(at, wide)],
+                slot_sem.at[0], slot_sem.at[1 + i], partner,
+            )
+
+    @pl.when(core == 0)
+    def _():
+        expert(kept)
+
+    @pl.when(core == 1)
+    def _():
+        eup_load.wait()
+        edn_load.wait()
+        wait_for(eup_v.at[:, pl.ds(0, moved)], units_sem.at[1])
+        wait_for(edn_v.at[pl.ds(0, moved)], units_sem.at[3])
+        expert(units + moved)
 
     wait_for(rhs.at[pl.ds(0, shared_units)], down_sem.at[1])
     wait_for(up_t.at[pl.ds(0, shared_units)], up_sem.at[1])
@@ -374,9 +462,14 @@
         own = own + t_recv[k]
     for h in range(HEADS):
         out_ref[:, h * HEAD_DIM : (h + 1) * HEAD_DIM] = own[h : h + 1, :].astype(BF16)
-    every_tile = pl.ds(0, TOKENS - 1)
-    for buf, sem in ((att, att_sem), (hid, hid_sem), (pro, pro_sem)):
-        wait_for(buf.at[every_tile], sem.at[0])
+    @pl.when(core == 0)
+    def _():
+        wait_for(eup_v.at[:, pl.ds(0, moved)], units_sem.at[0])
+        wait_for(edn_v.at[pl.ds(0, moved)], units_sem.at[2])
+
+    tiles_sent(att, att_sem)
+    wait_for(hid.at[pl.ds(0, TOKENS - 1)], hid_sem.at[0])
+    tiles_sent(pro, pro_sem)
     wait_for(rhs.at[pl.ds(0, shared_units)], down_sem.at[0])
     wait_for(up_t.at[pl.ds(0, shared_units)], up_sem.at[0])
     wait_for(rhs.at[pl.ds(placed_at, slots)], slot_sem.at[0])
@@ -400,6 +493,7 @@
     )
     d = query.shape[1]
     units = shared_up.shape[0]
+    wide_units = 2 * expert_up.shape[1] - expert_up.shape[1] // KEPT
     slots = TOKENS * 4 // 32
     tile = (TOKENS, HEADS, HEAD_DIM)
 
@@ -417,8 +511,8 @@
         own(ln_gain),
         pltpu.VMEM((2 * units + router.shape[0], d), BF16),
         pltpu.VMEM((2 * (units + slots), d), BF16),
-        own(expert_up),
-        own(expert_down),
+        pltpu.VMEM((d, wide_units), BF16),
+        pltpu.VMEM((wide_units, d), BF16),
         pltpu.VMEM(tile, BF16),
         pltpu.VMEM(tile, BF16),
         pltpu.VMEM((TOKENS, w_out.shape[0], TOKENS), BF16),
@@ -435,7 +529,7 @@
         pltpu.VMEM((RING - 1, HEADS, HEAD_DIM), F32),
         pltpu.VMEM((2 * (units + slots), TOKENS), BF16),
     ]
-    scratch += [dma((n,)) for n in (11, 16, 4, 16, 2, 2, 1 + PIECES, 2, 2)]
+    scratch += [dma((n,)) for n in (11, 27, 4, 27, 2, 2, 1 + PIECES, 2, 2, 4)]
     return pl.pallas_call(
         kernel,
         out_shape=jax.ShapeDtypeStruct((1, d), BF16),

time: 59.1 us -> 58.5 us (0.990)
  Pallas kernels: 57 us -> 56.2 us
    pallas_call x1, Pallas kernels: 57 us -> 56.2 us  [body(): pl.pallas_call(kernel, out_shape=jax.ShapeDtypeStruct((1, d), BF16), in_s...]
where the time goes in v7:
time: 58.5 us; the launch traced here: 58.2 us
  Pallas kernels  56.2 us (96%)
  local copies, waits for them, and re-layouts  1.3 us (2%)
  between operations  0.66 us (1%)
    pallas_call x1, Pallas kernels, body(): pl.pallas_call(kernel, out_shape=jax.ShapeDtypeStruct((1, d), BF16), in_s...  56.2 us
    unnamed x1, local copies, waits for them, and re-layouts  1.3 us

profile of v7, /device:TPU:514, one launch (start us, length us, event | category | flops | bytes accessed | tf_op | source)
XLA Modules:
  0.0 58.2 jit_solution(15358048658308722394)
XLA Ops:
  0.7 56.2 %decode_layer.1 = bf16[1,2048]{1,0:T(2,128)(2,1)} custom-call(bf16[1,2048]{1,0:T(2,128)(2,1)} %refs_0_.1, bf16[1,2048]{1,0:T(2,128)(2,1)} %refs_1_.1, bf16[1,2048]{1,0:T(2,128)(2,1)} %refs_2_.1, bf16[256,2048]{1,0:T(8,128)(2,1)} %bitcast.9, bf16[256,2048]{1,0:T(8,128)(2,1)} %bitcast.10, s32[1,1]{1,0:T(1,128)} %bitcast.8.refs_5_, bf16[1,2048]{1,0:T(2,128)(2,1)} %refs_6_.1, ...), custom_call_target="tpu_custom_call" | custom-call | tf_op jit(solution)/shard_map/decode_layer/pallas_call | solution.py:533
  56.9 1.3 %copy.18 = bf16[1,2048]{1,0:T(2,128)(2,1)} copy(bf16[1,2048]{1,0:T(2,128)(2,1)} %decode_layer.1) | data formatting | bytes 8192

commit v8 on v7

--- a/solution.py
+++ b/solution.py
@@ -532,7 +532,7 @@
     scratch += [dma((n,)) for n in (11, 27, 4, 27, 2, 2, 1 + PIECES, 2, 2, 4)]
     return pl.pallas_call(
         kernel,
-        out_shape=jax.ShapeDtypeStruct((1, d), BF16),
+        out_shape=pltpu.VMEM((1, d), BF16),
         in_specs=[pl.BlockSpec(memory_space=pl.ANY)] * 15,
         out_specs=pl.BlockSpec(memory_space=pltpu.VMEM),
         scratch_shapes=scratch,

time: 58.5 us -> 57.1 us (0.976)
  local copies, waits for them, and re-layouts: 1.3 us -> 0.6 us
  Pallas kernels: 56.2 us -> 55.6 us
    unnamed x1, local copies, waits for them, and re-layouts: 1.3 us -> 0.6 us
    pallas_call x1, Pallas kernels: 56.2 us -> 55.6 us  [body(): pl.pallas_call(kernel, out_shape=pltpu.VMEM((1, d), BF16), in_specs=[pl.B...]
where the time goes in v8:
time: 57.1 us; the launch traced here: 56.9 us
  Pallas kernels  55.6 us (97%)
  between operations  0.66 us (1%)
  local copies, waits for them, and re-layouts  0.6 us (1%)
    pallas_call x1, Pallas kernels, body(): pl.pallas_call(kernel, out_shape=pltpu.VMEM((1, d), BF16), in_specs=[pl.B...  55.6 us

profile of v8, /device:TPU:514, one launch (start us, length us, event | category | flops | bytes accessed | tf_op | source)
XLA Modules:
  0.0 56.9 jit_solution(7166742677345069696)
XLA Ops:
  0.7 55.6 %decode_layer.1 = bf16[1,2048]{1,0:T(2,128)(2,1)S(1)} custom-call(bf16[1,2048]{1,0:T(2,128)(2,1)} %refs_0_.1, bf16[1,2048]{1,0:T(2,128)(2,1)} %refs_1_.1, bf16[1,2048]{1,0:T(2,128)(2,1)} %refs_2_.1, bf16[256,2048]{1,0:T(8,128)(2,1)} %bitcast.9, bf16[256,2048]{1,0:T(8,128)(2,1)} %bitcast.10, s32[1,1]{1,0:T(1,128)} %bitcast.8.refs_5_, ...), custom_call_target="tpu_custom_call" | custom-call | tf_op jit(solution)/shard_map/decode_layer/pallas_call | solution.py:533
  56.3 0.6 %copy.17 = bf16[1,2048]{1,0:T(2,128)(2,1)} copy(bf16[1,2048]{1,0:T(2,128)(2,1)S(1)} %decode_layer.1) | data formatting | bytes 8192

commit v9 on v8

--- a/solution.py
+++ b/solution.py
@@ -352,10 +352,10 @@
     wo_load.wait()
     half_1 = projected(HALF)
     tiles_3(att, att_sem, 0)
-    steps_2(hid, hid_sem)
     half_0 = projected(0)
     pro[me] = jnp.concatenate([half_0, half_1], axis=1).astype(BF16)
     tiles_1(pro, pro_sem)
+    steps_2(hid, hid_sem)
     tiles_2(pro, pro_sem, [(0, OWN)] + [(color, k) for k in NEAR_FIRST for color in (1, 0)])
     steps_3(hid, hid_sem)
     steps_4(hid, hid_sem)

time: 57.1 us -> 57.2 us (level)
  no operation moved by 1% of the time
where the time goes in v9:
time: 57.2 us; the launch traced here: 57.1 us
  Pallas kernels  55.8 us (98%)
  between operations  0.66 us (1%)
  local copies, waits for them, and re-layouts  0.6 us (1%)
    pallas_call x1, Pallas kernels, body(): pl.pallas_call(kernel, out_shape=pltpu.VMEM((1, d), BF16), in_specs=[pl.B...  55.8 us

profile of v9, /device:TPU:514, one launch (start us, length us, event | category | flops | bytes accessed | tf_op | source)
XLA Modules:
  0.0 57.1 jit_solution(10924670352038096748)
XLA Ops:
  0.7 55.8 %decode_layer.1 = bf16[1,2048]{1,0:T(2,128)(2,1)S(1)} custom-call(bf16[1,2048]{1,0:T(2,128)(2,1)} %refs_0_.1, bf16[1,2048]{1,0:T(2,128)(2,1)} %refs_1_.1, bf16[1,2048]{1,0:T(2,128)(2,1)} %refs_2_.1, bf16[256,2048]{1,0:T(8,128)(2,1)} %bitcast.9, bf16[256,2048]{1,0:T(8,128)(2,1)} %bitcast.10, s32[1,1]{1,0:T(1,128)} %bitcast.8.refs_5_, ...), custom_call_target="tpu_custom_call" | custom-call | tf_op jit(solution)/shard_map/decode_layer/pallas_call | solution.py:533
  56.5 0.6 %copy.17 = bf16[1,2048]{1,0:T(2,128)(2,1)} copy(bf16[1,2048]{1,0:T(2,128)(2,1)S(1)} %decode_layer.1) | data formatting | bytes 8192
